TPU v7x, 128 devices: a whole 4x4x4 slice. The times are simulated.
128 devices in a mesh: seq: 16 (over z_hi, y, core), head: 8 (over x, z_lo).
Axes of the slice: x: 4, y: 4, z: 4 (z_hi: 2, z_lo: 2; z = z_hi * 2 + z_lo), core: 2. Of those that a mesh axis runs over, the one named last changes fastest.
Arguments:
- latent: bfloat16 [16, 1024, 2048], P('seq', None, 'head'), may hold values from -6 to 6
- modulation: float32 [9, 2048], replicated, may hold values from -3 to 3
- spatial_qkv: bfloat16 [3, 2048, 2048], P(None, None, 'head')
- spatial_out: bfloat16 [2048, 2048], P('head'), may hold values from -0.125 to 0.125
- temporal_qkv: bfloat16 [3, 2048, 2048], P(None, None, 'head')
- temporal_out: bfloat16 [2048, 2048], P('head'), may hold values from -0.125 to 0.125
- hidden_weight: bfloat16 [2048, 8192], P(None, 'head'), may hold values from -0.125 to 0.125
- output_weight: bfloat16 [8192, 2048], P('head'), may hold values from -0.0625 to 0.0625
Outputs:
- block_out: bfloat16 [16, 1024, 2048], P(None, 'seq', 'head')
All inputs are finite; a program needn't handle non-finite values.
Results may differ from a plain program's by a relative error of at most 0.009.
Values may be sent and summed in bfloat16 or wider, within the bound.
A program may use at most 128 MiB of HBM per device.

v0:
```python
import jax
import jax.numpy as jnp
from jax import lax
from jax.sharding import PartitionSpec as P

HD = 64


def split_up(shard, dim, devices):
    lengths = shard.shape
    blocks = shard.reshape(*lengths[:dim], devices, lengths[dim] // devices, *lengths[dim + 1 :])
    return jnp.moveaxis(blocks, dim, 0)


def sum_at_owner(shard, axis, dim):
    devices = lax.axis_size(axis)
    blocks = lax.all_to_all(split_up(shard, dim, devices), axis, 0, 0, tiled=True)
    return jnp.sum(blocks.astype(jnp.float32), axis=0)


def layer_norm(values):
    average = jnp.mean(values, axis=-1, keepdims=True)
    centred = values - average
    variance = jnp.mean(centred * centred, axis=-1, keepdims=True)
    return centred * lax.rsqrt(variance + 1e-06)


def modulate(stream, modulation, offset):
    normed = layer_norm(stream.astype(jnp.float32))
    return (normed * (1.0 + modulation[offset + 1]) + modulation[offset]).astype(jnp.bfloat16)


def attend(query, keys, values):
    scores = jnp.einsum(
        "glhd,gmhd->ghlm", query, keys, preferred_element_type=jnp.float32
    ) * HD ** (-0.5)
    attn_weights = jax.nn.softmax(scores, axis=-1).astype(jnp.bfloat16)
    return jnp.einsum(
        "ghlm,gmhd->glhd", attn_weights, values, preferred_element_type=jnp.float32
    ).astype(jnp.bfloat16)


def project_three(normed, weights):
    return [
        jnp.dot(normed, weights[member], preferred_element_type=jnp.float32).astype(jnp.bfloat16)
        for member in range(3)
    ]


def column_adder(columns, portion):
    return jnp.dot(portion, columns, preferred_element_type=jnp.float32)


def per_device(
    latent,
    modulation,
    spatial_qkv,
    spatial_out,
    temporal_qkv,
    temporal_out,
    hidden_weight,
    output_weight,
):
    width_local = latent.shape[2]
    heads_local = width_local // HD
    anchor = lax.axis_index("head") * width_local
    local_rows = lax.dynamic_slice_in_dim(modulation, anchor, width_local, 1)
    full_spatial = lax.all_gather(latent, "head", axis=2, tiled=True)
    normed = modulate(full_spatial, modulation, 0)
    frames_local = latent.shape[0]
    patches = latent.shape[1]
    query, keys, values = [
        member.reshape(frames_local, patches, heads_local, HD)
        for member in project_three(normed, spatial_qkv)
    ]
    spatial = lax.map(
        lambda triple: attend(triple[0][None], triple[1][None], triple[2][None])[0],
        (query, keys, values),
    )
    spatial = spatial.reshape(frames_local, patches, width_local)
    columns = lax.all_to_all(spatial_out, "head", split_axis=1, concat_axis=0, tiled=True)
    reduced = column_adder(columns, lax.all_gather(spatial, "head", axis=2, tiled=True))
    stream_one = (latent.astype(jnp.float32) + local_rows[2] * reduced).astype(jnp.bfloat16)
    stream_temporal = lax.all_to_all(stream_one, "seq", split_axis=1, concat_axis=0, tiled=True)
    full_temporal = lax.all_gather(stream_temporal, "head", axis=2, tiled=True)
    normed = modulate(full_temporal, modulation, 3)
    query, keys, values = project_three(normed, temporal_qkv)
    frames = stream_temporal.shape[0]
    patches_local = stream_temporal.shape[1]

    def to_groups(tensor):
        return jnp.transpose(tensor.reshape(frames, patches_local, heads_local, HD), (1, 0, 2, 3))

    temporal = attend(to_groups(query), to_groups(keys), to_groups(values))
    temporal = jnp.transpose(temporal, (1, 0, 2, 3)).reshape(frames, patches_local, width_local)
    columns = lax.all_to_all(temporal_out, "head", split_axis=1, concat_axis=0, tiled=True)
    reduced = column_adder(columns, lax.all_gather(temporal, "head", axis=2, tiled=True))
    stream_two = (stream_temporal.astype(jnp.float32) + local_rows[5] * reduced).astype(
        jnp.bfloat16
    )
    full_two = lax.all_gather(stream_two, "head", axis=2, tiled=True)
    normed = modulate(full_two, modulation, 6)
    pre_act = jnp.dot(normed, hidden_weight, preferred_element_type=jnp.float32)
    hidden = jax.nn.gelu(pre_act, approximate=True).astype(jnp.bfloat16)
    partial_sums = jnp.dot(hidden, output_weight, preferred_element_type=jnp.float32)
    reduced = sum_at_owner(partial_sums.astype(jnp.bfloat16), "head", 2)
    return (stream_two.astype(jnp.float32) + local_rows[8] * reduced).astype(jnp.bfloat16)


def solution(mesh):
    in_specs = (
        P("seq", None, "head"),
        P(),
        P(None, None, "head"),
        P("head", None),
        P(None, None, "head"),
        P("head", None),
        P(None, "head"),
        P("head", None),
    )
    out_specs = P(None, "seq", "head")
    return jax.shard_map(
        per_device, mesh=mesh, in_specs=in_specs, out_specs=out_specs, check_vma=False
    )
```

profile of v0, /device:TPU:8, one launch (start us, length us, event | category | flops | bytes accessed | tf_op | source)
XLA Modules:
  0.0 685.9 jit_solution(7628114898617417352)
XLA Ops:
  8.4 99.1 %all-gather.6.cloned.1.call-done = bf16[1,1024,2048]{2,1,0:T(8,128)(2,1)} async-done(((bf16[1,1024,256]{2,1,0:T(8,128)(2,1)}), bf16[1,1024,2048]{2,1,0:T(8,128)(2,1)}) %all-gather.6.cloned.1.call-update) | async-done | bytes 4194320 | tf_op jit(solution)/shard_map/all_gather | solution.py:68
  107.6 3.0 convert_reduce_fusion.2
  118.1 5.2 fusion.130
  123.3 8.1 %fusion.136 = f32[4,1024,1024]{1,2,0:T(8,128)} fusion(bf16[1024,4,64]{0,2,1:T(8,128)(2,1)S(1)} %bitcast.142, bf16[1024,4,64]{0,2,1:T(8,128)(2,1)S(1)} %bitcast.144), kind=kOutput, calls=%fused_computation.124 | convolution fusion | flops 536870912 | bytes 17825792 | tf_op jit(solution)/shard_map/while/body/eval_jaxpr/glhd,gmhd->ghlm/dot_general | solution.py:34
  131.4 16.0 %fusion.69 = bf16[4,64,1024]{2,1,0:T(8,128)(2,1)} fusion(bf16[1024,4,64]{0,2,1:T(8,128)(2,1)S(1)} %bitcast.162, f32[4,1024]{1,0:T(4,128)S(1)} %fusion.130, f32[4,1024,1024]{1,2,0:T(8,128)} %fusion.136), kind=kOutput, calls=%fused_computation.78 | convolution fusion | flops 558109696 | bytes 17842176 | tf_op jit(solution)/shard_map/while/body/eval_jaxpr/ghlm,gmhd->glhd/dot_general | solution.py:38
  148.7 5.7 all-to-all-start
  155.3 21.3 %all-to-all-done = bf16[256,8,256]{0,2,1:T(8,128)(2,1)S(1)} async-done(((bf16[256,8,256]{0,2,1:T(8,128)(2,1)}), bf16[256,8,256]{0,2,1:T(8,128)(2,1)S(1)}, u32[]{:S(2)}, u32[]{:S(2)}) %all-to-all-start) | async-done | bytes 1048608 | tf_op jit(solution)/shard_map/all_to_all | solution.py:81
  177.2 71.1 %all-gather.8.cloned.1.call-done = bf16[1,1024,2048]{1,2,0:T(8,128)(2,1)} async-done(((bf16[1,1024,256]{1,2,0:T(8,128)(2,1)}), bf16[1,1024,2048]{1,2,0:T(8,128)(2,1)}) %all-gather.8.cloned.1.call-update) | async-done | bytes 4194320 | tf_op jit(solution)/shard_map/all_gather | solution.py:82
  248.3 3.5 fusion.65
  253.1 3.8 reduce.6
  257.1 15.9 %all_to_all.55 = bf16[16,2,8192]{2,1,0:T(2,128)(2,1)S(1)} all-to-all(bf16[16,2,8192]{2,1,0:T(2,128)(2,1)S(1)} %reshape.181), channel_id=1, replica_groups=mesh['seq'=16,'head'=8] {'seq'}, dimensions={0} | all-to-all | bytes 1048576 | tf_op jit(solution)/shard_map/all_to_all | solution.py:84
  274.6 94.5 %all-gather.10.cloned.1.call-done = bf16[16,64,2048]{2,1,0:T(8,128)(2,1)} async-done(((bf16[16,64,256]{2,1,0:T(8,128)(2,1)}), bf16[16,64,2048]{2,1,0:T(8,128)(2,1)}) %all-gather.10.cloned.1.call-update) | async-done | bytes 4194320 | tf_op jit(solution)/shard_map/all_gather | solution.py:85
  369.2 3.0 convert_reduce_fusion.1
  373.9 3.0 convolution_convert_fusion.1
  377.2 4.2 convolution_convert_fusion.2
  381.9 5.0 convolution_convert_fusion.3
  389.2 3.3 fusion.131
  397.1 24.9 %all_to_all.56 = bf16[256,8,256]{2,0,1:T(8,128)(2,1)S(1)} all-to-all(bf16[256,8,256]{2,0,1:T(8,128)(2,1)S(1)} %bitcast.138), channel_id=1, replica_groups=mesh['seq'=16,'head'=8] {'head'}, dimensions={1} | all-to-all | bytes 2097152 | tf_op jit(solution)/shard_map/all_to_all | solution.py:96
  422.0 74.8 %all-gather.12.cloned.1.call-done = bf16[16,64,2048]{2,1,0:T(8,128)(2,1)} async-done(((bf16[16,64,256]{2,1,0:T(8,128)(2,1)}), bf16[16,64,2048]{2,1,0:T(8,128)(2,1)}) %all-gather.12.cloned.1.call-update) | async-done | bytes 4194320 | tf_op jit(solution)/shard_map/all_gather | solution.py:97
  496.8 4.2 fusion.68
  501.1 100.4 %all-gather.14.cloned.1.call-done = bf16[16,64,2048]{2,1,0:T(8,128)(2,1)} async-done(((bf16[16,64,256]{2,1,0:T(8,128)(2,1)}), bf16[16,64,2048]{2,1,0:T(8,128)(2,1)}) %all-gather.14.cloned.1.call-update) | async-done | bytes 4194320 | tf_op jit(solution)/shard_map/all_gather | solution.py:101
  601.5 3.0 convert_reduce_fusion
  606.2 15.3 %fusion.45 = bf16[16,64,2048]{2,1,0:T(8,128)(2,1)} fusion(bf16[1024,2048]{1,0:T(8,128)(2,1)} %param.15, bf16[16,64,2048]{2,1,0:T(8,128)(2,1)} %all-gather.14.cloned.1.call-done, bf16[2048,1024]{1,0:T(8,128)(2,1)} %param.14, f32[2048]{0:T(1024)S(1)} %bitcast.152, f32[2048]{0:T(1024)S(1)} %bitcast.151, f32[16,64]{1,0:T(8,128)S(1)} %add_rsqrt_fusion, ...), kind=kOutput, calls=%fused_computation.54 | convolution fusion | flops 8614051840 | bytes 16801792 | tf_op jit(solution)/shard_map/dot_general | solution.py:105
  624.3 52.6 %all_to_all.57 = bf16[8,16,64,256]{3,2,1,0:T(8,128)(2,1)S(1)} all-to-all(bf16[8,16,64,256]{3,2,1,0:T(8,128)(2,1)S(1)} %bitcast.133), channel_id=1, replica_groups=mesh['seq'=16,'head'=8] {'head'}, dimensions={0} | all-to-all | bytes 8388608 | tf_op jit(solution)/shard_map/all_to_all | solution.py:17
  (60 shorter events, 31.1 us)
Async XLA Ops:
  6.5 101.0 %all-gather.6.cloned.1.call-start = ((), (), s32[]{:S(2)}) async-start(), calls=%async_computation.4 | async-start | bytes 4718592 | tf_op jit(solution)/shard_map/all_gather | solution.py:68
  7.3 241.0 %all-gather.8.cloned.1.call-start = ((), (), s32[]{:S(2)}) async-start(), calls=%async_computation.5 | async-start | bytes 4718592 | tf_op jit(solution)/shard_map/all_gather | solution.py:82
  107.6 3.4 copy-start
  112.3 1.9 copy-start.8
  131.4 16.0 %copy-start.5 = (bf16[256,2048]{1,0:T(8,128)(2,1)S(1)}, bf16[256,2048]{1,0:T(8,128)(2,1)}, u32[]{:S(2)}) copy-start(bf16[256,2048]{1,0:T(8,128)(2,1)} %param.11) | copy-start | bytes 3145732
  147.4 100.9 %copy-start.7 = (bf16[1,1024,256]{2,1,0:T(8,128)(2,1)S(1)}, bf16[1,1024,256]{2,1,0:T(8,128)(2,1)}, u32[]{:S(2)}) copy-start(bf16[1,1024,256]{2,1,0:T(8,128)(2,1)} %param.8) | copy-start | bytes 1572868
  148.7 27.9 %all-to-all-start = ((bf16[256,8,256]{0,2,1:T(8,128)(2,1)}), bf16[256,8,256]{0,2,1:T(8,128)(2,1)S(1)}, u32[]{:S(2)}, u32[]{:S(2)}) async-start(bf16[256,8,256]{0,2,1:T(8,128)(2,1)} %bitcast.14), calls=%async_computation | async-start | bytes 2097152 | tf_op jit(solution)/shard_map/all_to_all | solution.py:81
  154.4 214.7 %all-gather.10.cloned.1.call-start = ((), (), s32[]{:S(2)}) async-start(), calls=%async_computation.6 | async-start | bytes 4718592 | tf_op jit(solution)/shard_map/all_gather | solution.py:85
  274.4 222.5 %all-gather.12.cloned.1.call-start = ((), (), s32[]{:S(2)}) async-start(), calls=%async_computation.7 | async-start | bytes 4718592 | tf_op jit(solution)/shard_map/all_gather | solution.py:97
  369.2 3.4 copy-start.1
  394.9 2.1 copy-start.6
  395.0 101.9 %copy-start.3 = (bf16[1,1024,256]{2,1,0:T(8,128)(2,1)S(1)}, bf16[1,1024,256]{2,1,0:T(8,128)(2,1)}, u32[]{:S(2)}) copy-start(bf16[1,1024,256]{2,1,0:T(8,128)(2,1)} %copy.55) | copy-start | bytes 1572868
  397.0 204.6 %all-gather.14.cloned.1.call-start = ((), (), s32[]{:S(2)}) async-start(), calls=%async_computation.8 | async-start | bytes 4718592 | tf_op jit(solution)/shard_map/all_gather | solution.py:101
  601.5 3.4 copy-start.2
  676.8 1.0 copy-start.4
Sparse Core Ops, SparseCore 0:
  8.9 98.6 all-gather.5
  147.5 100.7 all-gather.7
  274.5 94.6 all-gather.9
  397.1 99.6 all-gather.11
  501.2 100.2 all-gather.13
where the time goes:
time: 696 us; the launch traced here: 686 us
  waiting for transfers between devices  462 us (66%)
  blocking collectives  93.4 us (13%)
  matrix products  74.2 us (11%)
  other arithmetic  21.1 us (3%)
  local copies, waits for them, and re-layouts  15.2 us (2%)
  between operations  13.9 us (2%)
    all_gather x1, waiting for transfers between devices, per_device(): full_two = lax.all_gather(stream_two, 'head', axis=2, tiled=True)  100 us
    all_gather x1, waiting for transfers between devices, per_device(): full_spatial = lax.all_gather(latent, 'head', axis=2, tiled=True)  99.1 us
    all_gather x1, waiting for transfers between devices, per_device(): full_temporal = lax.all_gather(stream_temporal, 'head', axis=2, tiled=True)  94.5 us
    all_gather x1, waiting for transfers between devices, per_device(): lax.all_gather(temporal, 'head', axis=2, tiled=True)  74.8 us
    all_gather x1, waiting for transfers between devices, per_device(): lax.all_gather(spatial, 'head', axis=2, tiled=True)  71.1 us
    all_to_all x1, blocking collectives, sum_at_owner(): lax.all_to_all(split_up(shard, dim, devices), axis, 0, 0, tiled=True)  52.6 us
    all_to_all x1, blocking collectives, per_device(): lax.all_to_all(temporal_out, 'head', split_axis=1, concat_axis=0, tiled=T...  24.9 us
    all_to_all x1, waiting for transfers between devices, per_device(): lax.all_to_all(spatial_out, 'head', split_axis=1, concat_axis=0, tiled=True)  21.3 us
  transfers between devices with their start and end apart: 6, of which 6 were waited for; matrix products, arithmetic and copies ran while one was open for 1% of the time, Pallas kernels for 0%

commit v1 on v0

v1 whole, which is shorter than its diff:
```python
import functools

import jax
import jax.numpy as jnp
from jax import lax
from jax.experimental import pallas as pl
from jax.experimental.pallas import tpu as pltpu
from jax.sharding import PartitionSpec as P

MESH = pl.DeviceIdType.MESH
BF = jnp.bfloat16
F32 = jnp.float32
T = 1024
D = 2048
B = 256
VM = pltpu.VMEM
ANY = pl.BlockSpec(memory_space=pl.ANY)
INV = pl.BlockSpec(memory_space=pltpu.VMEM)


def rc(src, dst, ss, rs, dev):
    return pltpu.make_async_remote_copy(
        src_ref=src, dst_ref=dst, send_sem=ss, recv_sem=rs, device_id=dev, device_id_type=MESH
    )


class Place:
    def __init__(self):
        s, h = lax.axis_index("seq"), lax.axis_index("head")
        self.c, self.y, self.zh = lax.rem(s, 2), lax.rem(lax.div(s, 2), 4), lax.div(s, 8)
        self.x, self.zl = lax.div(h, 2), lax.rem(h, 2)
        self.z = self.zh * 2 + self.zl
        self.o = 1 - self.c
        self.row = (self.zh * 4 + self.y) * 2 + self.zl
        self.xr, self.xl, self.xf = [lax.rem(self.x + k, 4) for k in (1, 3, 2)]
        self.R = self.dev(self.xr, self.z, self.c)
        self.L = self.dev(self.xl, self.z, self.c)
        self.D = self.dev(self.x, self.z, self.o)
        self.U = self.dev(self.x, lax.rem(self.z + 1, 4), self.c)
        self.N = self.dev(self.x, lax.rem(self.z + 3, 4), self.c)
        self.S = ((self.zh * 4 + self.y) * 2 + self.o, self.x * 2 + 1 - self.zl)

    def dev(self, x, z, c):
        return ((lax.div(z, 2) * 4 + self.y) * 2 + c, x * 2 + lax.rem(z, 2))

    def row_dev(self, row):
        return (lax.div(row, 2) * 2 + self.c, self.x * 2 + lax.rem(row, 2))


def greet(devices):
    barrier = pltpu.get_barrier_semaphore()
    for device in devices:
        pl.semaphore_signal(barrier, inc=1, device_id=device, device_id_type=MESH)
    pl.semaphore_wait(barrier, len(devices))


def blk(x, c, width=B, off=0):
    return pl.ds(pl.multiple_of((x * 2 + c) * B + off, 128), width)


class Gather:
    KINDS = 9

    def __init__(self, p, full, rows, ss, rs):
        self.p, self.full, self.rows, self.ss, self.rs = p, full, rows, ss, rs
        x, c, o = p.x, p.c, p.o
        H = 128
        self.sent = [
            (blk(x, c), p.R), (blk(x, c), p.L), (blk(x, c), p.D),
            (blk(p.xl, c, H), p.R), (blk(p.xr, c, H, H), p.L),
            (blk(p.xl, c), p.D), (blk(p.xr, c), p.D),
            (blk(p.xf, c, H), p.D), (blk(p.xf, c, H, H), p.D),
        ]
        self.landed = [
            blk(p.xl, c), blk(p.xr, c), blk(x, o),
            blk(p.xf, c, H), blk(p.xf, c, H, H),
            blk(p.xl, o), blk(p.xr, o),
            blk(p.xf, o, H), blk(p.xf, o, H, H),
        ]

    def out(self, k, t):
        cols, dev = self.sent[k]
        ref = self.full.at[(*self.rows(t), cols)]
        return rc(ref, ref, self.ss.at[k, t], self.rs.at[k, t], dev)

    def got(self, k, t):
        ref = self.full.at[(*self.rows(t), self.landed[k])]
        rc(ref, ref, self.ss.at[k, t], self.rs.at[k, t], self.sent[k][1]).wait_recv()

    def own(self, t):
        for k in (0, 1, 2):
            self.out(k, t).start()

    def relay(self, t):
        self.got(0, t)
        self.out(3, t).start()
        self.out(5, t).start()
        self.got(1, t)
        self.out(4, t).start()
        self.out(6, t).start()

    def far(self, t):
        self.got(3, t)
        self.out(7, t).start()
        self.got(4, t)
        self.out(8, t).start()

    def arrive(self, t):
        for k in (2, 5, 6, 7, 8):
            self.got(k, t)

    def drain(self, t):
        for k in range(9):
            self.out(k, t).wait_send()


class Reduce:
    def __init__(self, p, ch, act, half, w, part, fs, fr, ns, nr, ss, rs):
        self.p, self.ch, self.act, self.half, self.w, self.part = p, ch, act, half, w, part
        self.fs, self.fr, self.ns, self.nr, self.ss, self.rs = fs, fr, ns, nr, ss, rs

    def r(self, t):
        return pl.ds(pl.multiple_of(t * self.ch, self.ch), self.ch)

    def copy(self, k, t):
        p, r = self.p, self.r(t)
        if k == 0:
            src, dst, dev = self.act.at[r, 0 : self.half], self.act.at[r, self.half : 2 * self.half], p.D
        elif k in (1, 2):
            src, dst, dev = self.fs.at[k - 1, r], self.fr.at[k - 1, r], (p.R, p.L)[k - 1]
        else:
            src, dst, dev = self.ns.at[k - 3, r], self.nr.at[k - 3, r], (p.R, p.L)[k - 3]
        return rc(src, dst, self.ss.at[k, t], self.rs.at[k, t], dev)

    def share(self, t):
        self.copy(0, t).start()

    def project(self, t):
        r = self.r(t)
        self.copy(0, t).wait_recv()
        out = jnp.dot(self.act[r, :], self.w[...], preferred_element_type=F32)
        self.fs[0, r] = out[:, 512:640].astype(BF)
        self.fs[1, r] = out[:, 640:768].astype(BF)
        self.copy(1, t).start()
        self.copy(2, t).start()
        self.part[r, 0:512] = out[:, 0:512]
        self.part[r, 512:768] = out[:, 768:1024]

    def near(self, t):
        r = self.r(t)
        self.copy(1, t).wait_recv()
        self.ns[0, r, 0:128] = (self.part[r, 256:384] + self.fr[0, r].astype(F32)).astype(BF)
        self.ns[0, r, 128:256] = self.part[r, 384:512].astype(BF)
        self.copy(3, t).start()
        self.copy(2, t).wait_recv()
        self.ns[1, r, 0:128] = self.part[r, 512:640].astype(BF)
        self.ns[1, r, 128:256] = (self.part[r, 640:768] + self.fr[1, r].astype(F32)).astype(BF)
        self.copy(4, t).start()

    def total(self, t):
        r = self.r(t)
        self.copy(3, t).wait_recv()
        self.copy(4, t).wait_recv()
        return self.part[r, 0:256] + self.nr[0, r].astype(F32) + self.nr[1, r].astype(F32)

    def drain(self, t):
        for k in range(5):
            self.copy(k, t).wait_send()


def reduce_scratch(nc, width):
    return [
        VM((T, width), BF), VM((width, 1024), BF), VM((T, 768), F32),
        VM((2, T, 128), BF), VM((2, T, 128), BF), VM((2, T, B), BF), VM((2, T, B), BF),
        pltpu.SemaphoreType.DMA((5, nc)), pltpu.SemaphoreType.DMA((5, nc)),
    ]


def normed(values, mod, row):
    v = values.astype(F32)
    v = v - jnp.mean(v, axis=-1, keepdims=True)
    v = v * lax.rsqrt(jnp.mean(v * v, axis=-1, keepdims=True) + 1e-06)
    return (v * (1.0 + mod[row + 1 : row + 2, :]) + mod[row : row + 1, :]).astype(BF)


def stages(n, *steps):
    last = max(lag for lag, _ in steps)

    def body(i, carry):
        for lag, function in steps:
            t = i - lag

            @pl.when((t >= 0) & (t < n))
            def _(t=t, function=function):
                function(t)

        return carry

    lax.fori_loop(0, n + last, body, 0)


def each(n, function):
    def body(i, carry):
        function(i)
        return carry

    lax.fori_loop(0, n, body, 0)


class QKV:
    def __init__(self, p, w, mine, theirs, ss, rs, ls):
        self.p, self.w, self.mine, self.theirs, self.ss, self.rs, self.ls = p, w, mine, theirs, ss, rs, ls

    def pieces(self):
        half = pl.ds(pl.multiple_of(self.p.c * 128, 128), 128)
        for j in range(3):
            yield j, self.ls.at[j], pltpu.make_async_copy(
                self.w.at[j, :, half], self.mine.at[:, j * 128 : j * 128 + 128], self.ls.at[j]
            )

    def sends(self):
        half = pl.ds(pl.multiple_of(self.p.c * 128, 128), 128)
        for j in range(3):
            for d, dev in enumerate((self.p.U, self.p.N)):
                yield rc(
                    self.w.at[j, d * 1024 : d * 1024 + 1024, half],
                    self.theirs.at[d * 1024 : d * 1024 + 1024, j * 128 : j * 128 + 128],
                    self.ss.at[j * 2 + d], self.rs.at[j * 2 + d], dev,
                )

    def start(self):
        for copy in self.sends():
            copy.start()
        for _, _, copy in self.pieces():
            copy.start()

    def wait_mine(self):
        for _, _, copy in self.pieces():
            copy.wait()

    def wait_theirs(self):
        for copy in self.sends():
            copy.wait_recv()

    def drain(self):
        for copy in self.sends():
            copy.wait_send()


class Out:
    def __init__(self, p, w, dst, rows, ss, rs, ls, stage=None):
        self.p, self.w, self.dst, self.rows, self.ss, self.rs, self.ls, self.stage = p, w, dst, rows, ss, rs, ls, stage

    def src(self, g, j):
        half = (self.p.c, self.p.o)[g]
        n = self.rows
        return self.w.at[pl.ds(pl.multiple_of(half * n, n), n), blk(lax.rem(self.p.x + j, 4), self.p.c)]

    def locals(self):
        n = self.rows
        for g in range(2):
            for j in range(4):
                yield pltpu.make_async_copy(
                    self.src(g, j), self.dst.at[2 * g * n : 2 * g * n + n, j * B : j * B + B], self.ls.at[g * 4 + j]
                )

    def sends(self):
        n = self.rows
        for g in range(2):
            for j in range(4):
                if self.stage is None:
                    dst = self.dst.at[2 * g * n + n : 2 * g * n + 2 * n, j * B : j * B + B]
                else:
                    dst = self.stage.at[g * n : g * n + n, j * B : j * B + B]
                yield rc(
                    self.src(g, j), dst,
                    self.ss.at[g * 4 + j], self.rs.at[g * 4 + j], (self.p.U, self.p.N)[g],
                )

    def wait_recv(self):
        for copy in self.sends():
            copy.wait_recv()

    def drain(self):
        for copy in self.sends():
            copy.wait_send()


DMA = pltpu.SemaphoreType.DMA
NC, CH = 8, 128


def flat_rows(t):
    return (pl.ds(pl.multiple_of(t * CH, CH), CH),)


def spatial_in(latent, mod, w, qkv, own, full, nrm, mine, theirs, gs, gr, ws, wr, wl, ls, ss, sr):
    p = Place()
    greet([p.L, p.R, p.D, p.U, p.N, p.S])
    gather = Gather(p, full, flat_rows, gs, gr)
    weights = QKV(p, w, mine, theirs, ws, wr, wl)
    here = blk(p.x, p.c)

    def keep(t):
        r = flat_rows(t)[0]
        return pltpu.make_async_copy(latent.at[0, r, :], full.at[r, here], ls.at[t])

    def swap(t):
        r = flat_rows(t)[0]
        return rc(latent.at[0, r, :], full.at[r, blk(p.x, p.o)], ss.at[t], sr.at[t], p.S)

    def landed(t):
        r = flat_rows(t)[0]
        return rc(latent.at[0, r, :], full.at[r, here], ss.at[t], sr.at[t], p.S)

    @pl.when(p.c == p.zl)
    def _():
        each(NC, lambda t: keep(t).start())

    @pl.when(p.c != p.zl)
    def _():
        each(NC, lambda t: swap(t).start())

    weights.start()

    def first(t):
        @pl.when(p.c == p.zl)
        def _():
            keep(t).wait()

        @pl.when(p.c != p.zl)
        def _():
            landed(t).wait_recv()

        gather.own(t)

    def compute(t):
        gather.arrive(t)
        r = flat_rows(t)[0]
        nrm[r, :] = normed(full[r, :], mod, 0)
        own[r, :] = full[r, here]

        @pl.when(t == 0)
        def _():
            weights.wait_mine()

        qkv[r, 0:384] = jnp.dot(nrm[r, :], mine[...], preferred_element_type=F32).astype(BF)

    stages(NC, (0, first), (1, gather.relay), (2, gather.far), (3, compute))
    weights.wait_theirs()

    def rest(t):
        r = flat_rows(t)[0]
        qkv[r, 384:768] = jnp.dot(nrm[r, :], theirs[...], preferred_element_type=F32).astype(BF)

    each(NC, rest)
    each(NC, gather.drain)

    @pl.when(p.c != p.zl)
    def _():
        each(NC, lambda t: swap(t).wait_send())

    weights.drain()


def lanes(rows):
    return lax.broadcasted_iota(jnp.int32, (rows, 128), 1)


def widen(qkv, vx):
    for pair in range(2):
        vx[pair, :, 0:128] = qkv[:, pair * 384 + 256 : pair * 384 + 384]
        vx[pair, :, 128:256] = jnp.ones((T, 128), BF)


def head_pair(q, k, v, mask):
    lane = lanes(q.shape[0])
    outs = []
    for a in range(2):
        qa = jnp.where((lane < 64) == (a == 0), q, jnp.zeros_like(q))
        s = lax.dot_general(qa, k, (((1,), (1,)), ((), ())), preferred_element_type=F32)
        if mask is not None:
            s = jnp.where(mask, s, -1e30)
        e = jnp.exp(s - jnp.max(s, axis=-1, keepdims=True)).astype(BF)
        o = jnp.dot(e, v, preferred_element_type=F32)
        outs.append(o[:, 0:128] / o[:, 128:256])
    return jnp.where(lane < 64, outs[0], outs[1]).astype(BF)


def attend_out(spatial, ch, gate_row, qkv, own, mod, w, extra, out, rider, *scratch):
    act, w2, part, fs, fr, ns, nr, rs_s, rs_r, vx, ws, wr, wl, es, er = scratch
    n = T // ch
    p = Place()
    greet([p.L, p.R, p.D, p.U, p.N])
    weights = Out(p, w, w2, 128, ws, wr, wl)
    reduce = Reduce(p, ch, act, 256, w2, part, fs, fr, ns, nr, rs_s, rs_r)
    for copy in weights.sends():
        copy.start()
    for copy in weights.locals():
        copy.start()
    if spatial:
        half = pl.ds(pl.multiple_of(p.c * 512, 512), 512)
        riders = [
            rc(
                extra.at[d * 1024 : d * 1024 + 1024, half], rider.at[d * 1024 : d * 1024 + 1024, :],
                es.at[d], er.at[d], (p.U, p.N)[d],
            )
            for d in range(2)
        ]
    else:
        riders = list(Out(p, extra, None, 512, es, er, None, rider).sends())
    for copy in riders:
        copy.start()
    widen(qkv, vx)
    if spatial:
        mask = None
    else:
        i = lax.broadcasted_iota(jnp.int32, (ch, ch), 0)
        j = lax.broadcasted_iota(jnp.int32, (ch, ch), 1)
        mask = lax.rem(i, 16) == lax.rem(j, 16)

    def heads(t):
        r = reduce.r(t)
        keys = slice(None) if spatial else r
        for pair in range(2):
            base = pair * 384
            q = qkv[r, base : base + 128] * jnp.array(0.125, BF)
            act[r, pair * 128 : pair * 128 + 128] = head_pair(
                q, qkv[keys, base + 128 : base + 256], vx[pair, keys, :], mask
            )
        reduce.share(t)

    def project(t):
        @pl.when(t == 0)
        def _():
            weights.wait_recv()
            for copy in weights.locals():
                copy.wait()

        reduce.project(t)

    gate = mod[gate_row : gate_row + 1, blk(p.x, p.c)]

    def finish(t):
        r = reduce.r(t)
        out[r, :] = (own[r, :].astype(F32) + gate * reduce.total(t)).astype(BF)

    stages(n, (0, heads), (1, project), (2, reduce.near), (3, finish))
    each(n, reduce.drain)
    weights.drain()
    for copy in riders:
        copy.wait()


def patch_rows(t):
    return (lax.div(t, 2), pl.ds(lax.rem(t, 2) * 8, 8), slice(None))


def temporal_in(stream, mod, w, qkv, own, full, nrm, mine, theirs, gs, gr, ws, wr, wl, ls, ss, sr):
    p = Place()
    peers = [p.row_dev(lax.rem(p.row + k, 16)) for k in range(1, 16)]
    greet([p.L, p.R, p.D] + peers)
    gather = Gather(p, full, patch_rows, gs, gr)
    weights = QKV(p, w, mine, theirs, ws, wr, wl)
    here = blk(p.x, p.c)

    def send(k):
        row = lax.rem(p.row + k, 16)
        return rc(
            stream.at[pl.ds(row * 4, 4), :, :], full.at[:, p.row, :, here],
            ss.at[k], sr.at[p.row], p.row_dev(row),
        )

    keep = pltpu.make_async_copy(stream.at[pl.ds(p.row * 4, 4), :, :], full.at[:, p.row, :, here], ls.at[0])
    each(15, lambda k: send(k + 1).start())
    keep.start()
    weights.start()

    def arrived(k):
        frame = lax.rem(p.row + k, 16)
        rc(
            stream.at[pl.ds(frame * 4, 4), :, :], full.at[:, frame, :, here],
            ss.at[k], sr.at[frame], p.row_dev(frame),
        ).wait_recv()

    keep.wait()
    each(15, lambda k: arrived(k + 1))

    def compute(t):
        gather.arrive(t)
        r = flat_rows(t)[0]
        index = patch_rows(t)
        nrm[r, :] = normed(full[(*index, slice(None))].reshape(CH, D), mod, 3)
        own[r, :] = full[(*index, here)].reshape(CH, B)

        @pl.when(t == 0)
        def _():
            weights.wait_mine()

        qkv[r, 0:384] = jnp.dot(nrm[r, :], mine[...], preferred_element_type=F32).astype(BF)

    stages(NC, (0, gather.own), (1, gather.relay), (2, gather.far), (3, compute))
    weights.wait_theirs()

    def rest(t):
        r = flat_rows(t)[0]
        qkv[r, 384:768] = jnp.dot(nrm[r, :], theirs[...], preferred_element_type=F32).astype(BF)

    each(NC, rest)
    each(NC, gather.drain)
    each(15, lambda k: send(k + 1).wait_send())
    weights.drain()


def mlp(stream, mod, hw, hw_p, ow, ow_p, out, full, w1, res, *scratch):
    act, w2, part, fs, fr, ns, nr, rs_s, rs_r, gs, gr, wl, ls, ss, sr = scratch
    p = Place()
    greet([p.L, p.R, p.D, p.S])
    gather = Gather(p, full, flat_rows, gs, gr)
    reduce = Reduce(p, CH, act, 1024, w2, part, fs, fr, ns, nr, rs_s, rs_r)
    here = blk(p.x, p.c)
    weights = Out(p, ow, w2, 512, None, None, wl)
    half = pl.ds(pl.multiple_of(p.c * 512, 512), 512)
    first = [
        pltpu.make_async_copy(hw.at[:, half], w1.at[:, 0:512], wl.at[8]),
        pltpu.make_async_copy(hw_p, w1.at[:, 512:1024], wl.at[9]),
    ]
    second = list(weights.locals()) + [
        pltpu.make_async_copy(ow_p.at[0:512, :], w2.at[512:1024, :], wl.at[10]),
        pltpu.make_async_copy(ow_p.at[512:1024, :], w2.at[1536:2048, :], wl.at[11]),
    ]

    def keep(t):
        r = flat_rows(t)[0]
        return pltpu.make_async_copy(stream.at[r, :], full.at[r, here], ls.at[t])

    each(NC, lambda t: keep(t).start())
    for copy in first + second:
        copy.start()

    def enter(t):
        keep(t).wait()
        gather.own(t)

    def hidden(t):
        @pl.when(t == 0)
        def _():
            for copy in first:
                copy.wait()

        gather.arrive(t)
        r = flat_rows(t)[0]
        h = jnp.dot(normed(full[r, :], mod, 6), w1[...], preferred_element_type=F32)
        h = 0.5 * h * (1.0 + jnp.tanh(0.7978845608028654 * (h + 0.044715 * (h * h * h))))
        act[r, 0:1024] = h.astype(BF)
        reduce.share(t)

    def project(t):
        @pl.when(t == 0)
        def _():
            for copy in second:
                copy.wait()

        reduce.project(t)

    gate = mod[8:9, here]

    def ends(t):
        src = res.at[pl.ds(t * 8, 8), :, :]
        dst = out.at[pl.ds(lax.rem(t, 2) * 8, 8), pl.ds(pl.multiple_of(lax.div(t, 2) * 16, 16), 16), :]
        return src, dst

    def put(t):
        return pltpu.make_async_copy(*ends(t), ls.at[t])

    def back(t):
        return rc(*ends(t), ss.at[t], sr.at[t], p.S)

    def finish(t):
        r = flat_rows(t)[0]
        value = full[r, here].astype(F32) + gate * reduce.total(t)
        res[pl.ds(t * 8, 8), :, :] = value.astype(BF).reshape(8, 16, B)

        @pl.when(p.c == p.zl)
        def _():
            put(t).start()

        @pl.when(p.c != p.zl)
        def _():
            back(t).start()

    stages(
        NC, (0, enter), (1, gather.relay), (2, gather.far), (3, hidden), (4, project), (5, reduce.near), (6, finish)
    )
    each(NC, gather.drain)
    each(NC, reduce.drain)

    @pl.when(p.c == p.zl)
    def _():
        each(NC, lambda t: put(t).wait())

    @pl.when(p.c != p.zl)
    def _():
        each(NC, lambda t: back(t).wait())


def call(kernel, name, ident, ins, outs, scratch, limit, cost):
    return pl.pallas_call(
        kernel,
        name=name,
        out_shape=[jax.ShapeDtypeStruct(shape, BF) for shape, _ in outs],
        in_specs=ins,
        out_specs=[spec for _, spec in outs],
        scratch_shapes=scratch,
        compiler_params=pltpu.CompilerParams(
            collective_id=ident, has_side_effects=True, vmem_limit_bytes=limit << 20
        ),
        cost_estimate=pl.CostEstimate(flops=cost, bytes_accessed=1 << 24, transcendentals=0),
    )


def gather_scratch(full):
    return [
        VM(full, BF), VM((T, D), BF), VM((D, 384), BF), VM((D, 384), BF),
        DMA((9, NC)), DMA((9, NC)), DMA((6,)), DMA((6,)), DMA((3,)), DMA((NC,)),
    ]


def per_device(latent, mod, sqkv, so, tqkv, to, hw, ow):
    qkv_shape, block = (T, 768), (T, B)
    qkv, own = call(
        spatial_in, "spatial_in", 0, [ANY, INV, ANY], [(qkv_shape, INV), (block, INV)],
        gather_scratch((T, D)) + [DMA((NC,)), DMA((NC,))], 40, 10**10,
    )(latent, mod, sqkv)

    def attend(spatial, ch, row, ident, qkv, own, w, extra):
        n = T // ch
        rider = ((D, 512), ANY) if spatial else ((1024, 1024), ANY)
        return call(
            functools.partial(attend_out, spatial, ch, row), "spatial_out" if spatial else "temporal_out", ident,
            [INV, INV, INV, ANY, ANY], [(block, INV), rider],
            reduce_scratch(n, 512)
            + [VM((2, T, B), BF), DMA((8,)), DMA((8,)), DMA((8,)), DMA((8,)), DMA((8,))],
            40, 10**10,
        )(qkv, own, mod, w, extra)

    one, hw_p = attend(True, 128, 2, 1, qkv, own, so, hw)
    qkv, own = call(
        temporal_in, "temporal_in", 2, [INV, INV, ANY], [(qkv_shape, INV), (block, INV)],
        gather_scratch((4, 16, 16, D)) + [DMA((16,)), DMA((16,))], 40, 10**10,
    )(one.reshape(64, 16, B), mod, tqkv)
    two, ow_p = attend(False, 256, 5, 3, qkv, own, to, ow)
    (out,) = call(
        mlp, "mlp", 4, [INV, INV, ANY, ANY, ANY, ANY], [((16, 64, B), ANY)],
        [VM((T, D), BF), VM((D, 1024), BF), VM((64, 16, B), BF)]
        + reduce_scratch(NC, 2048)
        + [DMA((9, NC)), DMA((9, NC)), DMA((12,)), DMA((NC,)), DMA((NC,)), DMA((NC,))],
        48, 2 * 10**10,
    )(two, mod, hw, hw_p, ow, ow_p)
    return out


def solution(mesh):
    in_specs = (
        P("seq", None, "head"), P(), P(None, None, "head"), P("head", None),
        P(None, None, "head"), P("head", None), P(None, "head"), P("head", None),
    )
    return jax.shard_map(
        per_device, mesh=mesh, in_specs=in_specs, out_specs=P(None, "seq", "head"), check_vma=False
    )
```

time: 696 us -> 218 us (0.31)
  the two profiles are of different devices: /device:TPU:8 before, /device:TPU:1 now
where the time goes in v1:
time: 218 us
  Pallas kernels  213 us (98%)
  local copies, waits for them, and re-layouts  4.97 us (2%)
    pallas_call x2, Pallas kernels, attend(): call(functools.partial(attend_out, spatial, ch, row), 'spatial_out' if sp...  72.7 us
    pallas_call x1, Pallas kernels, per_device(): call(mlp, 'mlp', 4, [INV, INV, ANY, ANY, ANY, ANY], [((16, 64, B), ANY)],...  53.7 us
    pallas_call x1, Pallas kernels, per_device(): call(temporal_in, 'temporal_in', 2, [INV, INV, ANY], [(qkv_shape, INV), (...  46.9 us
    pallas_call x1, Pallas kernels, per_device(): call(spatial_in, 'spatial_in', 0, [ANY, INV, ANY], [(qkv_shape, INV), (bl...  39.4 us
    unnamed x19, local copies, waits for them, and re-layouts  4.97 us

profile of v1, /device:TPU:1, one launch (start us, length us, event | category | flops | bytes accessed | tf_op | source)
XLA Modules:
  0.0 217.8 jit_solution(5711613650533998137)
XLA Ops:
  0.0 0.0 copy-start
  0.0 0.0 copy-start.2
  0.0 2.0 copy-done.2
  2.0 0.0 copy-start.6
  2.0 1.2 copy-done.6
  3.2 0.0 copy-start.7
  3.3 0.9 copy-done.7
  4.2 0.0 copy-start.4
  4.2 0.0 copy-start.8
  4.2 39.4 %spatial_in.1 = (bf16[1024,768]{1,0:T(8,128)(2,1)S(1)}, bf16[1024,256]{1,0:T(8,128)(2,1)S(1)}) custom-call(bf16[1,1024,256]{2,1,0:T(8,128)(2,1)S(1)} %copy-done.6, f32[9,2048]{1,0:T(8,128)S(1)} %copy-done.7, bf16[3,2048,256]{2,1,0:T(8,128)(2,1)S(1)} %copy-done.2), custom_call_target="tpu_custom_call" | custom-call | flops 10000000000 | bytes 16777216 | tf_op jit(solution)/shard_map/spatial_in/pallas_call | solution.py:631
  43.6 0.0 copy-done
  43.6 0.0 copy-done.4
  43.6 0.0 copy-done.8
  43.6 0.0 copy-start.3
  43.6 39.5 %spatial_out.1 = (bf16[1024,256]{1,0:T(8,128)(2,1)S(1)}, bf16[2048,512]{1,0:T(8,128)(2,1)S(1)}) custom-call(bf16[1024,768]{1,0:T(8,128)(2,1)S(1)} %get-tuple-element.13.qkv, bf16[1024,256]{1,0:T(8,128)(2,1)S(1)} %get-tuple-element.14.own, f32[9,2048]{1,0:T(8,128)S(1)} %copy-done.8, bf16[256,2048]{1,0:T(8,128)(2,1)S(1)} %copy-done.4, ...), custom_call_target="tpu_custom_call" | custom-call | flops 10000000000 | bytes 16777216 | tf_op jit(solution)/shard_map/spatial_out/pallas_call | solution.py:639
  83.1 0.0 copy-done.3
  83.1 0.0 copy-start.1
  83.2 0.0 copy-start.5
  83.2 46.9 %temporal_in.1 = (bf16[1024,768]{1,0:T(8,128)(2,1)S(1)}, bf16[1024,256]{1,0:T(8,128)(2,1)S(1)}) custom-call(bf16[64,16,256]{2,1,0:T(8,128)(2,1)S(1)} %bitcast.1, f32[9,2048]{1,0:T(8,128)S(1)} %copy-done.8, bf16[3,2048,256]{2,1,0:T(8,128)(2,1)S(1)} %copy-done.3), custom_call_target="tpu_custom_call" | custom-call | flops 10000000000 | bytes 16777216 | tf_op jit(solution)/shard_map/temporal_in/pallas_call | solution.py:648
  130.1 0.0 copy-done.1
  130.1 0.0 copy-done.5
  130.1 33.2 %temporal_out.1 = (bf16[1024,256]{1,0:T(8,128)(2,1)S(1)}, bf16[1024,1024]{1,0:T(8,128)(2,1)S(1)}) custom-call(bf16[1024,768]{1,0:T(8,128)(2,1)S(1)} %get-tuple-element.16.qkv, bf16[1024,256]{1,0:T(8,128)(2,1)S(1)} %get-tuple-element.17.own, f32[9,2048]{1,0:T(8,128)S(1)} %copy-done.8, bf16[256,2048]{1,0:T(8,128)(2,1)S(1)} %copy-done.5, ...), custom_call_target="tpu_custom_call" | custom-call | flops 10000000000 | bytes 16777216 | tf_op jit(solution)/shard_map/temporal_out/pallas_call | solution.py:639
  163.3 53.7 %mlp.1 = bf16[16,64,256]{2,1,0:T(8,128)(2,1)S(1)} custom-call(bf16[1024,256]{1,0:T(8,128)(2,1)S(1)} %get-tuple-element.18.stream, f32[9,2048]{1,0:T(8,128)S(1)} %copy-done.8, bf16[2048,1024]{1,0:T(8,128)(2,1)} %hw.1, bf16[2048,512]{1,0:T(8,128)(2,1)S(1)} %get-tuple-element.19.hw_p, bf16[1024,2048]{1,0:T(8,128)(2,1)} %ow.1, ...), custom_call_target="tpu_custom_call" | custom-call | flops 20000000000 | bytes 16777216 | tf_op jit(solution)/shard_map/mlp/pallas_call | solution.py:653
  217.0 0.8 copy.10
Async XLA Ops:
  0.0 43.6 %copy-start = (bf16[2048,1024]{1,0:T(8,128)(2,1)S(1)}, bf16[2048,1024]{1,0:T(8,128)(2,1)}, u32[]{:S(2)}) copy-start(bf16[2048,1024]{1,0:T(8,128)(2,1)} %hw.1) | copy-start | bytes 12582916
  0.0 2.0 copy-start.2
  2.0 1.2 copy-start.6
  3.2 0.9 copy-start.7
  4.2 39.4 %copy-start.4 = (bf16[256,2048]{1,0:T(8,128)(2,1)S(1)}, bf16[256,2048]{1,0:T(8,128)(2,1)}, u32[]{:S(2)}) copy-start(bf16[256,2048]{1,0:T(8,128)(2,1)} %w.5) | copy-start | bytes 3145732
  4.2 39.4 %copy-start.8 = (f32[9,2048]{1,0:T(8,128)S(1)}, f32[9,2048]{1,0:T(8,128)}, u32[]{:S(2)}) copy-start(f32[9,2048]{1,0:T(8,128)} %mod.9) | copy-start | bytes 221188
  43.6 39.5 %copy-start.3 = (bf16[3,2048,256]{2,1,0:T(8,128)(2,1)S(1)}, bf16[3,2048,256]{2,1,0:T(8,128)(2,1)}, u32[]{:S(2)}) copy-start(bf16[3,2048,256]{2,1,0:T(8,128)(2,1)} %w.6) | copy-start | bytes 9437188
  83.1 47.0 %copy-start.1 = (bf16[1024,2048]{1,0:T(8,128)(2,1)S(1)}, bf16[1024,2048]{1,0:T(8,128)(2,1)}, u32[]{:S(2)}) copy-start(bf16[1024,2048]{1,0:T(8,128)(2,1)} %ow.1) | copy-start | bytes 12582916
  83.2 47.0 %copy-start.5 = (bf16[256,2048]{1,0:T(8,128)(2,1)S(1)}, bf16[256,2048]{1,0:T(8,128)(2,1)}, u32[]{:S(2)}) copy-start(bf16[256,2048]{1,0:T(8,128)(2,1)} %w.7) | copy-start | bytes 3145732

commit v2 on v1

--- a/solution.py
+++ b/solution.py
@@ -14,7 +14,7 @@
 D = 2048
 B = 256
 VM = pltpu.VMEM
-ANY = pl.BlockSpec(memory_space=pl.ANY)
+ANY = pl.BlockSpec(memory_space=pltpu.MemorySpace.HBM)
 INV = pl.BlockSpec(memory_space=pltpu.VMEM)
 
 
@@ -346,7 +346,7 @@
 
         qkv[r, 0:384] = jnp.dot(nrm[r, :], mine[...], preferred_element_type=F32).astype(BF)
 
-    stages(NC, (0, first), (1, gather.relay), (2, gather.far), (3, compute))
+    stages(NC, (0, first), (2, gather.relay), (4, gather.far), (6, compute))
     weights.wait_theirs()
 
     def rest(t):
@@ -445,7 +445,7 @@
         r = reduce.r(t)
         out[r, :] = (own[r, :].astype(F32) + gate * reduce.total(t)).astype(BF)
 
-    stages(n, (0, heads), (1, project), (2, reduce.near), (3, finish))
+    stages(n, (0, heads), *((2, project), (4, reduce.near), (6, finish)) if spatial else ((1, project), (2, reduce.near), (3, finish)))
     each(n, reduce.drain)
     weights.drain()
     for copy in riders:
@@ -499,7 +499,7 @@
 
         qkv[r, 0:384] = jnp.dot(nrm[r, :], mine[...], preferred_element_type=F32).astype(BF)
 
-    stages(NC, (0, gather.own), (1, gather.relay), (2, gather.far), (3, compute))
+    stages(NC, (0, gather.own), (3, gather.relay), (5, gather.far), (6, compute))
     weights.wait_theirs()
 
     def rest(t):
@@ -590,7 +590,7 @@
             back(t).start()
 
     stages(
-        NC, (0, enter), (1, gather.relay), (2, gather.far), (3, hidden), (4, project), (5, reduce.near), (6, finish)
+        NC, (0, enter), (3, gather.relay), (5, gather.far), (6, hidden), (7, project), (9, reduce.near), (11, finish)
     )
     each(NC, gather.drain)
     each(NC, reduce.drain)

time: 218 us -> 195 us (0.89)
  Pallas kernels: 213 us -> 190 us
    pallas_call x2, Pallas kernels: 72.7 us -> 64.3 us  [attend(): call(functools.partial(attend_out, spatial, ch, row), 'spatial_out' if sp...]
    pallas_call x1, Pallas kernels: 53.7 us -> 46.1 us  [per_device(): call(mlp, 'mlp', 4, [INV, INV, ANY, ANY, ANY, ANY], [((16, 64, B), ANY)],...]
    pallas_call x1, Pallas kernels: 46.9 us -> 43 us  [per_device(): call(temporal_in, 'temporal_in', 2, [INV, INV, ANY], [(qkv_shape, INV), (...]
    pallas_call x1, Pallas kernels: 39.4 us -> 36.1 us  [per_device(): call(spatial_in, 'spatial_in', 0, [ANY, INV, ANY], [(qkv_shape, INV), (bl...]
where the time goes in v2:
time: 195 us
  Pallas kernels  190 us (97%)
  local copies, waits for them, and re-layouts  4.97 us (3%)
    pallas_call x2, Pallas kernels, attend(): call(functools.partial(attend_out, spatial, ch, row), 'spatial_out' if sp...  64.3 us
    pallas_call x1, Pallas kernels, per_device(): call(mlp, 'mlp', 4, [INV, INV, ANY, ANY, ANY, ANY], [((16, 64, B), ANY)],...  46.1 us
    pallas_call x1, Pallas kernels, per_device(): call(temporal_in, 'temporal_in', 2, [INV, INV, ANY], [(qkv_shape, INV), (...  43 us
    pallas_call x1, Pallas kernels, per_device(): call(spatial_in, 'spatial_in', 0, [ANY, INV, ANY], [(qkv_shape, INV), (bl...  36.1 us
    unnamed x19, local copies, waits for them, and re-layouts  4.97 us

profile of v2, /device:TPU:1, one launch (start us, length us, event | category | flops | bytes accessed | tf_op | source)
XLA Modules:
  0.0 194.6 jit_solution(2642688196715355374)
XLA Ops:
  0.0 0.0 copy-start
  0.0 0.0 copy-start.2
  0.0 2.0 %copy-done.2 = bf16[3,2048,256]{2,1,0:T(8,128)(2,1)S(1)} copy-done((bf16[3,2048,256]{2,1,0:T(8,128)(2,1)S(1)}, bf16[3,2048,256]{2,1,0:T(8,128)(2,1)}, u32[]{:S(2)}) %copy-start.2) | copy-done | bytes 3145752
  2.0 0.0 copy-start.6
  2.0 1.2 copy-done.6
  3.2 0.0 copy-start.7
  3.3 0.9 copy-done.7
  4.2 0.0 copy-start.4
  4.2 0.0 copy-start.8
  4.2 36.1 %spatial_in.1 = (bf16[1024,768]{1,0:T(8,128)(2,1)S(1)}, bf16[1024,256]{1,0:T(8,128)(2,1)S(1)}) custom-call(bf16[1,1024,256]{2,1,0:T(8,128)(2,1)S(1)} %copy-done.6, f32[9,2048]{1,0:T(8,128)S(1)} %copy-done.7, bf16[3,2048,256]{2,1,0:T(8,128)(2,1)S(1)} %copy-done.2), custom_call_target="tpu_custom_call" | custom-call | flops 10000000000 | bytes 16777216 | tf_op jit(solution)/shard_map/spatial_in/pallas_call | solution.py:631
  40.3 0.0 copy-done
  40.3 0.0 copy-done.4
  40.3 0.0 copy-done.8
  40.3 0.0 copy-start.3
  40.4 32.1 %spatial_out.1 = (bf16[1024,256]{1,0:T(8,128)(2,1)S(1)}, bf16[2048,512]{1,0:T(8,128)(2,1)S(1)}) custom-call(bf16[1024,768]{1,0:T(8,128)(2,1)S(1)} %get-tuple-element.13.qkv, bf16[1024,256]{1,0:T(8,128)(2,1)S(1)} %get-tuple-element.14.own, f32[9,2048]{1,0:T(8,128)S(1)} %copy-done.8, bf16[256,2048]{1,0:T(8,128)(2,1)S(1)} %copy-done.4, ...), custom_call_target="tpu_custom_call" | custom-call | flops 10000000000 | bytes 16777216 | tf_op jit(solution)/shard_map/spatial_out/pallas_call | solution.py:639
  72.5 0.0 copy-done.3
  72.5 0.0 copy-start.1
  72.5 0.0 copy-start.5
  72.5 43.0 %temporal_in.1 = (bf16[1024,768]{1,0:T(8,128)(2,1)S(1)}, bf16[1024,256]{1,0:T(8,128)(2,1)S(1)}) custom-call(bf16[64,16,256]{2,1,0:T(8,128)(2,1)S(1)} %bitcast.1, f32[9,2048]{1,0:T(8,128)S(1)} %copy-done.8, bf16[3,2048,256]{2,1,0:T(8,128)(2,1)S(1)} %copy-done.3), custom_call_target="tpu_custom_call" | custom-call | flops 10000000000 | bytes 16777216 | tf_op jit(solution)/shard_map/temporal_in/pallas_call | solution.py:648
  115.5 0.0 copy-done.1
  115.5 0.0 copy-done.5
  115.5 32.2 %temporal_out.1 = (bf16[1024,256]{1,0:T(8,128)(2,1)S(1)}, bf16[1024,1024]{1,0:T(8,128)(2,1)S(1)}) custom-call(bf16[1024,768]{1,0:T(8,128)(2,1)S(1)} %get-tuple-element.16.qkv, bf16[1024,256]{1,0:T(8,128)(2,1)S(1)} %get-tuple-element.17.own, f32[9,2048]{1,0:T(8,128)S(1)} %copy-done.8, bf16[256,2048]{1,0:T(8,128)(2,1)S(1)} %copy-done.5, ...), custom_call_target="tpu_custom_call" | custom-call | flops 10000000000 | bytes 16777216 | tf_op jit(solution)/shard_map/temporal_out/pallas_call | solution.py:639
  147.8 46.1 %mlp.1 = bf16[16,64,256]{2,1,0:T(8,128)(2,1)S(1)} custom-call(bf16[1024,256]{1,0:T(8,128)(2,1)S(1)} %get-tuple-element.18.stream, f32[9,2048]{1,0:T(8,128)S(1)} %copy-done.8, bf16[2048,1024]{1,0:T(8,128)(2,1)} %hw.1, bf16[2048,512]{1,0:T(8,128)(2,1)S(1)} %get-tuple-element.19.hw_p, bf16[1024,2048]{1,0:T(8,128)(2,1)} %ow.1, ...), custom_call_target="tpu_custom_call" | custom-call | flops 20000000000 | bytes 16777216 | tf_op jit(solution)/shard_map/mlp/pallas_call | solution.py:653
  193.8 0.8 copy.10
Async XLA Ops:
  0.0 40.3 %copy-start = (bf16[2048,1024]{1,0:T(8,128)(2,1)S(1)}, bf16[2048,1024]{1,0:T(8,128)(2,1)}, u32[]{:S(2)}) copy-start(bf16[2048,1024]{1,0:T(8,128)(2,1)} %hw.1) | copy-start | bytes 12582916
  0.0 2.0 %copy-start.2 = (bf16[3,2048,256]{2,1,0:T(8,128)(2,1)S(1)}, bf16[3,2048,256]{2,1,0:T(8,128)(2,1)}, u32[]{:S(2)}) copy-start(bf16[3,2048,256]{2,1,0:T(8,128)(2,1)} %w.4) | copy-start | bytes 9437188
  2.0 1.2 copy-start.6
  3.2 0.9 copy-start.7
  4.2 36.2 %copy-start.4 = (bf16[256,2048]{1,0:T(8,128)(2,1)S(1)}, bf16[256,2048]{1,0:T(8,128)(2,1)}, u32[]{:S(2)}) copy-start(bf16[256,2048]{1,0:T(8,128)(2,1)} %w.5) | copy-start | bytes 3145732
  4.2 36.2 %copy-start.8 = (f32[9,2048]{1,0:T(8,128)S(1)}, f32[9,2048]{1,0:T(8,128)}, u32[]{:S(2)}) copy-start(f32[9,2048]{1,0:T(8,128)} %mod.9) | copy-start | bytes 221188
  40.3 32.1 %copy-start.3 = (bf16[3,2048,256]{2,1,0:T(8,128)(2,1)S(1)}, bf16[3,2048,256]{2,1,0:T(8,128)(2,1)}, u32[]{:S(2)}) copy-start(bf16[3,2048,256]{2,1,0:T(8,128)(2,1)} %w.6) | copy-start | bytes 9437188
  72.5 43.0 %copy-start.1 = (bf16[1024,2048]{1,0:T(8,128)(2,1)S(1)}, bf16[1024,2048]{1,0:T(8,128)(2,1)}, u32[]{:S(2)}) copy-start(bf16[1024,2048]{1,0:T(8,128)(2,1)} %ow.1) | copy-start | bytes 12582916
  72.5 43.0 %copy-start.5 = (bf16[256,2048]{1,0:T(8,128)(2,1)S(1)}, bf16[256,2048]{1,0:T(8,128)(2,1)}, u32[]{:S(2)}) copy-start(bf16[256,2048]{1,0:T(8,128)(2,1)} %w.7) | copy-start | bytes 3145732

commit v3 on v2

v3 whole, which is shorter than its diff:
```python
import functools

import jax
import jax.numpy as jnp
from jax import lax
from jax.experimental import pallas as pl
from jax.experimental.pallas import tpu as pltpu
from jax.sharding import PartitionSpec as P

MESH = pl.DeviceIdType.MESH
BF = jnp.bfloat16
F32 = jnp.float32
T = 1024
D = 2048
B = 256
VM = pltpu.VMEM
ANY = pl.BlockSpec(memory_space=pltpu.MemorySpace.HBM)
INV = pl.BlockSpec(memory_space=pltpu.VMEM)


def rc(src, dst, ss, rs, dev):
    return pltpu.make_async_remote_copy(
        src_ref=src, dst_ref=dst, send_sem=ss, recv_sem=rs, device_id=dev, device_id_type=MESH
    )


class Place:
    def __init__(self):
        s, h = lax.axis_index("seq"), lax.axis_index("head")
        self.c, self.y, self.zh = lax.rem(s, 2), lax.rem(lax.div(s, 2), 4), lax.div(s, 8)
        self.x, self.zl = lax.div(h, 2), lax.rem(h, 2)
        self.z = self.zh * 2 + self.zl
        self.o = 1 - self.c
        self.row = (self.zh * 4 + self.y) * 2 + self.zl
        self.xr, self.xl, self.xf = [lax.rem(self.x + k, 4) for k in (1, 3, 2)]
        self.R = self.dev(self.xr, self.z, self.c)
        self.L = self.dev(self.xl, self.z, self.c)
        self.D = self.dev(self.x, self.z, self.o)
        self.U = self.dev(self.x, lax.rem(self.z + 1, 4), self.c)
        self.N = self.dev(self.x, lax.rem(self.z + 3, 4), self.c)
        self.S = ((self.zh * 4 + self.y) * 2 + self.o, self.x * 2 + 1 - self.zl)

    def dev(self, x, z, c):
        return ((lax.div(z, 2) * 4 + self.y) * 2 + c, x * 2 + lax.rem(z, 2))

    def row_dev(self, row):
        return (lax.div(row, 2) * 2 + self.c, self.x * 2 + lax.rem(row, 2))


def greet(devices):
    barrier = pltpu.get_barrier_semaphore()
    for device in devices:
        pl.semaphore_signal(barrier, inc=1, device_id=device, device_id_type=MESH)
    pl.semaphore_wait(barrier, len(devices))


def blk(x, c, width=B, off=0):
    return pl.ds(pl.multiple_of((x * 2 + c) * B + off, 128), width)


class Gather:
    KINDS = 9

    def __init__(self, p, full, rows, ss, rs):
        self.p, self.full, self.rows, self.ss, self.rs = p, full, rows, ss, rs
        x, c, o = p.x, p.c, p.o
        H = 128
        self.sent = [
            (blk(x, c), p.R), (blk(x, c), p.L), (blk(x, c), p.D),
            (blk(p.xl, c, H), p.R), (blk(p.xr, c, H, H), p.L),
            (blk(p.xl, c), p.D), (blk(p.xr, c), p.D),
            (blk(p.xf, c, H), p.D), (blk(p.xf, c, H, H), p.D),
        ]
        self.landed = [
            blk(p.xl, c), blk(p.xr, c), blk(x, o),
            blk(p.xf, c, H), blk(p.xf, c, H, H),
            blk(p.xl, o), blk(p.xr, o),
            blk(p.xf, o, H), blk(p.xf, o, H, H),
        ]

    def out(self, k, t):
        cols, dev = self.sent[k]
        ref = self.full.at[(*self.rows(t), cols)]
        return rc(ref, ref, self.ss.at[k, t], self.rs.at[k, t], dev)

    def got(self, k, t):
        ref = self.full.at[(*self.rows(t), self.landed[k])]
        rc(ref, ref, self.ss.at[k, t], self.rs.at[k, t], self.sent[k][1]).wait_recv()

    def own(self, t):
        for k in (0, 1, 2):
            self.out(k, t).start()

    def relay(self, t):
        self.got(0, t)
        self.out(3, t).start()
        self.out(5, t).start()
        self.got(1, t)
        self.out(4, t).start()
        self.out(6, t).start()

    def far(self, t):
        self.got(3, t)
        self.out(7, t).start()
        self.got(4, t)
        self.out(8, t).start()

    def arrive(self, t):
        for k in (2, 5, 6, 7, 8):
            self.got(k, t)

    def drain(self, t):
        for k in range(9):
            self.out(k, t).wait_send()


class Reduce:
    def __init__(self, p, ch, act, half, w, part, fs, fr, ns, nr, ss, rs):
        self.p, self.ch, self.act, self.half, self.w, self.part = p, ch, act, half, w, part
        self.fs, self.fr, self.ns, self.nr, self.ss, self.rs = fs, fr, ns, nr, ss, rs

    def r(self, t):
        return pl.ds(pl.multiple_of(t * self.ch, self.ch), self.ch)

    def copy(self, k, t):
        p, r = self.p, self.r(t)
        if k == 0:
            src, dst, dev = self.act.at[r, 0 : self.half], self.act.at[r, self.half : 2 * self.half], p.D
        elif k in (1, 2):
            src, dst, dev = self.fs.at[k - 1, r], self.fr.at[k - 1, r], (p.R, p.L)[k - 1]
        else:
            src, dst, dev = self.ns.at[k - 3, r], self.nr.at[k - 3, r], (p.R, p.L)[k - 3]
        return rc(src, dst, self.ss.at[k, t], self.rs.at[k, t], dev)

    def share(self, t):
        self.copy(0, t).start()

    def project(self, t):
        r = self.r(t)
        self.copy(0, t).wait_recv()
        out = jnp.dot(self.act[r, :], self.w[...], preferred_element_type=F32)
        self.fs[0, r] = out[:, 512:640].astype(BF)
        self.fs[1, r] = out[:, 640:768].astype(BF)
        self.copy(1, t).start()
        self.copy(2, t).start()
        self.part[r, 0:512] = out[:, 0:512]
        self.part[r, 512:768] = out[:, 768:1024]

    def near(self, t):
        r = self.r(t)
        self.copy(1, t).wait_recv()
        self.ns[0, r, 0:128] = (self.part[r, 256:384] + self.fr[0, r].astype(F32)).astype(BF)
        self.ns[0, r, 128:256] = self.part[r, 384:512].astype(BF)
        self.copy(3, t).start()
        self.copy(2, t).wait_recv()
        self.ns[1, r, 0:128] = self.part[r, 512:640].astype(BF)
        self.ns[1, r, 128:256] = (self.part[r, 640:768] + self.fr[1, r].astype(F32)).astype(BF)
        self.copy(4, t).start()

    def total(self, t):
        r = self.r(t)
        self.copy(3, t).wait_recv()
        self.copy(4, t).wait_recv()
        return self.part[r, 0:256] + self.nr[0, r].astype(F32) + self.nr[1, r].astype(F32)

    def drain(self, t):
        for k in range(5):
            self.copy(k, t).wait_send()


def normed(values, mod, row):
    v = values.astype(F32)
    v = v - jnp.mean(v, axis=-1, keepdims=True)
    v = v * lax.rsqrt(jnp.mean(v * v, axis=-1, keepdims=True) + 1e-06)
    return (v * (1.0 + mod[row + 1 : row + 2, :]) + mod[row : row + 1, :]).astype(BF)


def stages(n, *steps):
    last = max(lag for lag, _ in steps)

    def body(i, carry):
        for lag, function in steps:
            t = i - lag

            @pl.when((t >= 0) & (t < n))
            def _(t=t, function=function):
                function(t)

        return carry

    lax.fori_loop(0, n + last, body, 0)


def each(n, function):
    def body(i, carry):
        function(i)
        return carry

    lax.fori_loop(0, n, body, 0)


class QKV:
    def __init__(self, p, w, mine, theirs, ss, rs, ls):
        self.p, self.w, self.mine, self.theirs, self.ss, self.rs, self.ls = p, w, mine, theirs, ss, rs, ls
        self.half = pl.ds(pl.multiple_of(p.c * 128, 128), 128)

    def locals(self):
        return [
            pltpu.make_async_copy(self.w.at[j, :, self.half], self.mine.at[:, j * 128 : j * 128 + 128], self.ls.at[j])
            for j in range(3)
        ]

    def piece(self, i):
        for d, dev in enumerate((self.p.U, self.p.N)):
            rows = pl.ds(pl.multiple_of(d * 1024 + i * 128, 128), 128)
            for j in range(3):
                rc(
                    self.w.at[j, rows, self.half], self.theirs.at[rows, j * 128 : j * 128 + 128],
                    self.ss.at[d], self.rs.at[d], dev,
                ).start()

    def whole(self, d):
        ref = self.theirs.at[d * 1024 : d * 1024 + 1024, :]
        return rc(ref, ref, self.ss.at[d], self.rs.at[d], (self.p.U, self.p.N)[d])


class Out:
    def __init__(self, p, w, dst, rows, ss, rs, ls):
        self.p, self.w, self.dst, self.rows, self.ss, self.rs, self.ls = p, w, dst, rows, ss, rs, ls

    def src(self, g, j, first, count):
        start = (self.p.c, self.p.o)[g] * self.rows + first
        return self.w.at[pl.ds(pl.multiple_of(start, 128), count), blk(lax.rem(self.p.x + j, 4), self.p.c)]

    def locals(self):
        n = self.rows
        return [
            pltpu.make_async_copy(
                self.src(g, j, 0, n), self.dst.at[2 * g * n : 2 * g * n + n, j * B : j * B + B], self.ls.at[g * 4 + j]
            )
            for g in range(2)
            for j in range(4)
        ]

    def piece(self, i):
        n = self.rows
        per = n // 128
        j, first = lax.div(i, per), lax.rem(i, per) * 128
        for g, dev in enumerate((self.p.U, self.p.N)):
            rows = pl.ds(pl.multiple_of((2 * g + 1) * n + first, 128), 128)
            rc(
                self.src(g, j, first, 128), self.dst.at[rows, pl.ds(pl.multiple_of(j * B, B), B)],
                self.ss.at[g], self.rs.at[g], dev,
            ).start()

    def whole(self, g):
        n = self.rows
        ref = self.dst.at[(2 * g + 1) * n : (2 * g + 2) * n, :]
        return rc(ref, ref, self.ss.at[g], self.rs.at[g], (self.p.U, self.p.N)[g])


class Hidden:
    def __init__(self, p, w, dst, ss, rs, ls):
        self.p, self.w, self.dst, self.ss, self.rs, self.ls = p, w, dst, ss, rs, ls
        self.half = pl.ds(pl.multiple_of(p.c * 512, 512), 512)

    def locals(self):
        return [pltpu.make_async_copy(self.w.at[:, self.half], self.dst.at[:, 0:512], self.ls.at[0])]

    def piece(self, i):
        for d, dev in enumerate((self.p.U, self.p.N)):
            rows = pl.ds(pl.multiple_of(d * 1024 + i * 64, 64), 64)
            rc(
                self.w.at[rows, self.half], self.dst.at[rows, 512:1024], self.ss.at[d], self.rs.at[d], dev
            ).start()

    def whole(self, d):
        ref = self.dst.at[d * 1024 : d * 1024 + 1024, 512:1024]
        return rc(ref, ref, self.ss.at[d], self.rs.at[d], (self.p.U, self.p.N)[d])


def ready(weights):
    for d in range(2):
        weights.whole(d).wait_recv()
    for copy in weights.locals():
        copy.wait()


DMA = pltpu.SemaphoreType.DMA
NC, CH = 8, 128


def rows_of(t):
    return pl.ds(pl.multiple_of(t * CH, CH), CH)


def flat_rows(t):
    return (rows_of(t),)


def spatial_in(latent, mod, w, qkv, own, full, nrm, mine, theirs, gs, gr, ws, wr, wl, ls, ss, sr):
    p = Place()
    greet([p.L, p.R, p.D, p.U, p.N, p.S])
    gather = Gather(p, full, flat_rows, gs, gr)
    weights = QKV(p, w, mine, theirs, ws, wr, wl)
    here = blk(p.x, p.c)

    def keep(t):
        r = rows_of(t)
        return pltpu.make_async_copy(latent.at[r, :], full.at[r, here], ls.at[t])

    def swap(t):
        r = rows_of(t)
        return rc(latent.at[r, :], full.at[r, blk(p.x, p.o)], ss.at[t], sr.at[t], p.S)

    def landed(t):
        r = rows_of(t)
        return rc(latent.at[r, :], full.at[r, here], ss.at[t], sr.at[t], p.S)

    @pl.when(p.c == p.zl)
    def _():
        each(NC, lambda t: keep(t).start())

    @pl.when(p.c != p.zl)
    def _():
        each(NC, lambda t: swap(t).start())

    each(NC, weights.piece)
    for copy in weights.locals():
        copy.start()

    def first(t):
        @pl.when(p.c == p.zl)
        def _():
            keep(t).wait()

        @pl.when(p.c != p.zl)
        def _():
            landed(t).wait_recv()

        gather.own(t)

    def compute(t):
        gather.arrive(t)
        r = rows_of(t)
        nrm[r, :] = normed(full[r, :], mod, 0)
        own[r, :] = full[r, here]

        @pl.when(t == 0)
        def _():
            for copy in weights.locals():
                copy.wait()

        qkv[r, 0:384] = jnp.dot(nrm[r, :], mine[...], preferred_element_type=F32).astype(BF)

    stages(NC, (0, first), (2, gather.relay), (4, gather.far), (6, compute))
    for d in range(2):
        weights.whole(d).wait_recv()

    def rest(t):
        r = rows_of(t)
        qkv[r, 384:768] = jnp.dot(nrm[r, :], theirs[...], preferred_element_type=F32).astype(BF)

    each(NC, rest)
    each(NC, gather.drain)

    @pl.when(p.c != p.zl)
    def _():
        each(NC, lambda t: swap(t).wait_send())

    for d in range(2):
        weights.whole(d).wait_send()


def lanes(rows):
    return lax.broadcasted_iota(jnp.int32, (rows, 128), 1)


def head_pair(q, k, v, mask):
    lane = lanes(q.shape[0])
    outs = []
    for a in range(2):
        qa = jnp.where((lane < 64) == (a == 0), q, jnp.zeros_like(q))
        s = lax.dot_general(qa, k, (((1,), (1,)), ((), ())), preferred_element_type=F32)
        if mask is not None:
            s = jnp.where(mask, s, -1e30)
        e = jnp.exp(s - jnp.max(s, axis=-1, keepdims=True)).astype(BF)
        o = jnp.dot(e, v, preferred_element_type=F32)
        outs.append(o[:, 0:128] / o[:, 128:256])
    return jnp.where(lane < 64, outs[0], outs[1]).astype(BF)


PROJECT, NEAR, FINISH = 2, 4, 6
ENTER, RELAY, FAR, COMPUTE = 9, 11, 13, 15
PROJECT2, NEAR2, FINISH2 = 17, 19, 21
RELAY2, FAR2, COMPUTE2 = 23, 25, 27
PROJECT3, NEAR3, FINISH3 = 29, 31, 33


def tail(
    qkv, own, mod, so, tw, to, hw, ow, out,
    vx, ws, one, full1, mine, theirs, wt, full2, w1, w2, res, part,
    a1, fs1, fr1, ns1, nr1, a2, fs2, fr2, ns2, nr2, a3, fs3, fr3, ns3, nr3,
    s1, v1, s2, v2, s3, v3, g1, h1, g2, h2,
    ps, pr, qs, qr, us, ur, hs, hr, os, orr, pl_, ql, ul, hl, ol, xs, xr, ls, ss, sr,
):
    p = Place()
    greet([p.L, p.R, p.D, p.S] + [p.row_dev(lax.rem(p.row + k, 16)) for k in range(1, 16)])
    here = blk(p.x, p.c)
    wso = Out(p, so, ws, 128, ps, pr, pl_)
    wtq = QKV(p, tw, mine, theirs, qs, qr, ql)
    wto = Out(p, to, wt, 128, us, ur, ul)
    whi = Hidden(p, hw, w1, hs, hr, hl)
    wou = Out(p, ow, w2, 512, os, orr, ol)
    r1 = Reduce(p, CH, a1, 256, ws, part, fs1, fr1, ns1, nr1, s1, v1)
    r2 = Reduce(p, CH, a2, 256, wt, part, fs2, fr2, ns2, nr2, s2, v2)
    r3 = Reduce(p, CH, a3, 1024, w2, part, fs3, fr3, ns3, nr3, s3, v3)
    gat1 = Gather(p, full1, flat_rows, g1, h1)
    gat2 = Gather(p, full2, flat_rows, g2, h2)

    each(4, wso.piece)
    for weights in (wso, wtq, wto, whi, wou):
        for copy in weights.locals():
            copy.start()
    for pair in range(2):
        vx[pair, :, 0:128] = qkv[:, pair * 384 + 256 : pair * 384 + 384]
        vx[pair, :, 128:256] = jnp.ones((T, 128), BF)

    def heads(t):
        r = rows_of(t)
        for pair in range(2):
            base = pair * 384
            q = qkv[r, base : base + 128] * jnp.array(0.125, BF)
            a1[r, pair * 128 : pair * 128 + 128] = head_pair(q, qkv[:, base + 128 : base + 256], vx[pair], None)
        r1.share(t)

    def project1(t):
        @pl.when(t == 0)
        def _():
            ready(wso)

        r1.project(t)

    def eight(t, row):
        return pl.ds(pl.multiple_of(t * CH + row * 8, 8), 8)

    def cross(k, t):
        row = lax.rem(p.row + k, 16)
        return rc(one.at[eight(t, row), :], full1.at[eight(t, p.row), here], xs.at[k, t], xr.at[p.row, t], p.row_dev(row))

    def stay(t):
        return pltpu.make_async_copy(one.at[eight(t, p.row), :], full1.at[eight(t, p.row), here], xr.at[p.row, t])

    def finish1(t):
        r = rows_of(t)
        gate = mod[2:3, here]
        one[r, :] = (own[r, :].astype(F32) + gate * r1.total(t)).astype(BF)
        each(15, lambda k: cross(k + 1, t).start())
        stay(t).start()

    def enter1(t):
        def arrived(k):
            row = lax.rem(p.row + k, 16)
            rc(
                one.at[eight(t, row), :], full1.at[eight(t, row), here], xs.at[k, t], xr.at[row, t], p.row_dev(row)
            ).wait_recv()

        each(15, lambda k: arrived(k + 1))
        stay(t).wait()
        gat1.own(t)

    i = lax.broadcasted_iota(jnp.int32, (CH, CH), 0)
    j = lax.broadcasted_iota(jnp.int32, (CH, CH), 1)
    same = lax.rem(i, 8) == lax.rem(j, 8)

    def temporal(t):
        @pl.when(t == 0)
        def _():
            ready(wtq)

        gat1.arrive(t)
        r = rows_of(t)
        n = normed(full1[r, :], mod, 3)
        for pair, w in enumerate((mine, theirs)):
            y = jnp.dot(n, w[...], preferred_element_type=F32).astype(BF)
            v = jnp.concatenate([y[:, 256:384], jnp.ones((CH, 128), BF)], axis=1)
            a2[r, pair * 128 : pair * 128 + 128] = head_pair(
                y[:, 0:128] * jnp.array(0.125, BF), y[:, 128:256], v, same
            )
        r2.share(t)

    def project2(t):
        @pl.when(t == 0)
        def _():
            ready(wto)

        r2.project(t)

    def finish2(t):
        r = rows_of(t)
        gate = mod[5:6, here]
        full2[r, here] = (full1[r, here].astype(F32) + gate * r2.total(t)).astype(BF)
        gat2.own(t)

    def hidden(t):
        @pl.when(t == 0)
        def _():
            ready(whi)

        gat2.arrive(t)
        r = rows_of(t)
        h = jnp.dot(normed(full2[r, :], mod, 6), w1[...], preferred_element_type=F32)
        h = 0.5 * h * (1.0 + jnp.tanh(0.7978845608028654 * (h + 0.044715 * (h * h * h))))
        a3[r, 0:1024] = h.astype(BF)
        r3.share(t)

    def project3(t):
        @pl.when(t == 0)
        def _():
            ready(wou)

        r3.project(t)

    def put(t):
        r = rows_of(t)
        return pltpu.make_async_copy(res.at[r, :], out.at[r, :], ls.at[t])

    def back(t):
        r = rows_of(t)
        return rc(res.at[r, :], out.at[r, :], ss.at[t], sr.at[t], p.S)

    def finish3(t):
        r = rows_of(t)
        gate = mod[8:9, here]
        res[r, :] = (full2[r, here].astype(F32) + gate * r3.total(t)).astype(BF)

        @pl.when(p.c == p.zl)
        def _():
            put(t).start()

        @pl.when(p.c != p.zl)
        def _():
            back(t).start()

    def steps(*entries):
        def body(i, carry):
            for first, count, function in entries:

                @pl.when((i >= first) & (i < first + count))
                def _(t=i - first, function=function):
                    function(t)

            return carry

        lax.fori_loop(0, NC + FINISH3, body, 0)

    def twice(piece):
        def run(i):
            piece(2 * i)
            piece(2 * i + 1)

        return run

    steps(
        (0, 8, wtq.piece), (8, 4, wto.piece), (12, 8, twice(whi.piece)), (20, 8, twice(wou.piece)),
        (FINISH, NC, finish1), (ENTER, NC, enter1), (RELAY, NC, gat1.relay), (FAR, NC, gat1.far),
        (NEAR, NC, r1.near), (NEAR2, NC, r2.near), (NEAR3, NC, r3.near),
        (FINISH2, NC, finish2), (RELAY2, NC, gat2.relay), (FAR2, NC, gat2.far), (FINISH3, NC, finish3),
        (PROJECT, NC, project1), (PROJECT2, NC, project2), (PROJECT3, NC, project3),
        (0, NC, heads), (COMPUTE, NC, temporal), (COMPUTE2, NC, hidden),
    )

    def drain(t):
        for stage in (r1, r2, r3, gat1, gat2):
            stage.drain(t)
        each(15, lambda k: cross(k + 1, t).wait_send())

    each(NC, drain)
    for weights in (wso, wtq, wto, whi, wou):
        for d in range(2):
            weights.whole(d).wait_send()

    @pl.when(p.c == p.zl)
    def _():
        each(NC, lambda t: put(t).wait())

    @pl.when(p.c != p.zl)
    def _():
        each(NC, lambda t: back(t).wait())


def call(kernel, name, ident, ins, outs, scratch, limit, cost):
    return pl.pallas_call(
        kernel,
        name=name,
        out_shape=[jax.ShapeDtypeStruct(shape, BF) for shape, _ in outs],
        in_specs=ins,
        out_specs=[spec for _, spec in outs],
        scratch_shapes=scratch,
        compiler_params=pltpu.CompilerParams(
            collective_id=ident, has_side_effects=True, vmem_limit_bytes=limit << 20
        ),
        cost_estimate=pl.CostEstimate(flops=cost, bytes_accessed=1 << 24, transcendentals=0),
    )


def input_scratch():
    return [
        VM((T, D), BF), VM((T, D), BF), VM((D, 384), BF), VM((D, 384), BF),
        DMA((9, NC)), DMA((9, NC)), DMA((2,)), DMA((2,)), DMA((3,)), DMA((NC,)), DMA((NC,)), DMA((NC,)),
    ]


def tail_scratch():
    def reduce(width):
        return [VM((T, width), BF), VM((2, T, 128), BF), VM((2, T, 128), BF), VM((2, T, B), BF), VM((2, T, B), BF)]

    pair = [DMA((2,)), DMA((2,))]
    return (
        [VM((2, T, B), BF), VM((512, 1024), BF), VM((T, B), BF), VM((T, D), BF), VM((D, 384), BF), VM((D, 384), BF)]
        + [VM((512, 1024), BF), VM((T, D), BF), VM((D, 1024), BF), VM((D, 1024), BF), VM((T, B), BF), VM((T, 768), F32)]
        + reduce(512) + reduce(512) + reduce(2048)
        + [DMA((5, NC))] * 6 + [DMA((9, NC))] * 4
        + pair * 5 + [DMA((8,)), DMA((3,)), DMA((8,)), DMA((1,)), DMA((8,))]
        + [DMA((16, NC)), DMA((16, NC)), DMA((NC,)), DMA((NC,)), DMA((NC,))]
    )


def per_device(latent, mod, sqkv, so, tqkv, to, hw, ow):
    tokens = latent.reshape(16, 8, 8, B).transpose(1, 0, 2, 3).reshape(T, B)
    qkv, own = call(
        spatial_in, "spatial_in", 0, [ANY, INV, ANY], [((T, 768), INV), ((T, B), INV)], input_scratch(), 60, 10**10
    )(tokens, mod, sqkv)
    (out,) = call(
        tail, "tail", 1, [INV, INV, INV] + [ANY] * 5, [((T, B), ANY)], tail_scratch(), 60, 4 * 10**10
    )(qkv, own, mod, so, tqkv, to, hw, ow)
    return out.reshape(8, 16, 8, B).transpose(1, 0, 2, 3).reshape(16, 64, B)


def solution(mesh):
    in_specs = (
        P("seq", None, "head"), P(), P(None, None, "head"), P("head", None),
        P(None, None, "head"), P("head", None), P(None, "head"), P("head", None),
    )
    return jax.shard_map(
        per_device, mesh=mesh, in_specs=in_specs, out_specs=P(None, "seq", "head"), check_vma=False
    )
```

time: 195 us -> 169 us (0.87)
  Pallas kernels: 190 us -> 165 us
    pallas_call x5 -> x2, Pallas kernels: 190 us -> 165 us  [the longest x1 126 us: per_device(): call(tail, 'tail', 1, [INV, INV, INV] + [ANY] * 5, [((T, B), ANY)], tail_...]
    unnamed x19 -> x0, local copies, waits for them, and re-layouts: 4.97 us -> none
where the time goes in v3:
time: 169 us
  Pallas kernels  165 us (98%)
  local copies, waits for them, and re-layouts  3.76 us (2%)
    pallas_call x1, Pallas kernels, per_device(): call(tail, 'tail', 1, [INV, INV, INV] + [ANY] * 5, [((T, B), ANY)], tail_...  126 us
    pallas_call x1, Pallas kernels, per_device(): call(spatial_in, 'spatial_in', 0, [ANY, INV, ANY], [((T, 768), INV), ((T,...  38.5 us

profile of v3, /device:TPU:1, one launch (start us, length us, event | category | flops | bytes accessed | tf_op | source)
XLA Modules:
  0.0 168.5 jit_solution(6423134471469881279)
XLA Ops:
  0.0 1.9 %copy.9 = bf16[16,8,8,256]{3,2,0,1:T(8,128)(2,1)} copy(bf16[16,8,8,256]{3,2,1,0:T(8,128)(2,1)} %bitcast.10) | data formatting | bytes 1048576 | tf_op jit(solution)/shard_map/reshape | solution.py:630
  1.9 38.5 %spatial_in.1 = (bf16[1024,768]{1,0:T(8,128)(2,1)}, bf16[1024,256]{1,0:T(8,128)(2,1)}) custom-call(bf16[1024,256]{1,0:T(8,128)(2,1)} %bitcast.11, f32[9,2048]{1,0:T(8,128)} %mod.3, bf16[3,2048,256]{2,1,0:T(8,128)(2,1)} %w.1), custom_call_target="tpu_custom_call" | custom-call | flops 10000000000 | bytes 16777216 | tf_op jit(solution)/shard_map/spatial_in/pallas_call | solution.py:631
  40.4 126.3 %tail.1 = bf16[1024,256]{1,0:T(8,128)(2,1)} custom-call(bf16[1024,768]{1,0:T(8,128)(2,1)} %get-tuple-element.7.qkv, bf16[1024,256]{1,0:T(8,128)(2,1)} %get-tuple-element.8.own, f32[9,2048]{1,0:T(8,128)} %mod.3, bf16[256,2048]{1,0:T(8,128)(2,1)} %so.1, bf16[3,2048,256]{2,1,0:T(8,128)(2,1)} %tw.1, bf16[256,2048]{1,0:T(8,128)(2,1)} %to.1, ...), custom_call_target="tpu_custom_call" | custom-call | flops 40000000000 | bytes 16777216 | tf_op jit(solution)/shard_map/tail/pallas_call | solution.py:634
  166.6 1.9 %copy.12 = bf16[16,8,8,256]{3,2,1,0:T(8,128)(2,1)} copy(bf16[16,8,8,256]{3,2,0,1:T(8,128)(2,1)} %bitcast.12) | data formatting | bytes 1048576 | tf_op jit(solution)/shard_map/transpose | solution.py:637

commit v4 on v3

--- a/solution.py
+++ b/solution.py
@@ -175,22 +175,6 @@
     return (v * (1.0 + mod[row + 1 : row + 2, :]) + mod[row : row + 1, :]).astype(BF)
 
 
-def stages(n, *steps):
-    last = max(lag for lag, _ in steps)
-
-    def body(i, carry):
-        for lag, function in steps:
-            t = i - lag
-
-            @pl.when((t >= 0) & (t < n))
-            def _(t=t, function=function):
-                function(t)
-
-        return carry
-
-    lax.fori_loop(0, n + last, body, 0)
-
-
 def each(n, function):
     def body(i, carry):
         function(i)
@@ -296,80 +280,6 @@
 
 def flat_rows(t):
     return (rows_of(t),)
-
-
-def spatial_in(latent, mod, w, qkv, own, full, nrm, mine, theirs, gs, gr, ws, wr, wl, ls, ss, sr):
-    p = Place()
-    greet([p.L, p.R, p.D, p.U, p.N, p.S])
-    gather = Gather(p, full, flat_rows, gs, gr)
-    weights = QKV(p, w, mine, theirs, ws, wr, wl)
-    here = blk(p.x, p.c)
-
-    def keep(t):
-        r = rows_of(t)
-        return pltpu.make_async_copy(latent.at[r, :], full.at[r, here], ls.at[t])
-
-    def swap(t):
-        r = rows_of(t)
-        return rc(latent.at[r, :], full.at[r, blk(p.x, p.o)], ss.at[t], sr.at[t], p.S)
-
-    def landed(t):
-        r = rows_of(t)
-        return rc(latent.at[r, :], full.at[r, here], ss.at[t], sr.at[t], p.S)
-
-    @pl.when(p.c == p.zl)
-    def _():
-        each(NC, lambda t: keep(t).start())
-
-    @pl.when(p.c != p.zl)
-    def _():
-        each(NC, lambda t: swap(t).start())
-
-    each(NC, weights.piece)
-    for copy in weights.locals():
-        copy.start()
-
-    def first(t):
-        @pl.when(p.c == p.zl)
-        def _():
-            keep(t).wait()
-
-        @pl.when(p.c != p.zl)
-        def _():
-            landed(t).wait_recv()
-
-        gather.own(t)
-
-    def compute(t):
-        gather.arrive(t)
-        r = rows_of(t)
-        nrm[r, :] = normed(full[r, :], mod, 0)
-        own[r, :] = full[r, here]
-
-        @pl.when(t == 0)
-        def _():
-            for copy in weights.locals():
-                copy.wait()
-
-        qkv[r, 0:384] = jnp.dot(nrm[r, :], mine[...], preferred_element_type=F32).astype(BF)
-
-    stages(NC, (0, first), (2, gather.relay), (4, gather.far), (6, compute))
-    for d in range(2):
-        weights.whole(d).wait_recv()
-
-    def rest(t):
-        r = rows_of(t)
-        qkv[r, 384:768] = jnp.dot(nrm[r, :], theirs[...], preferred_element_type=F32).astype(BF)
-
-    each(NC, rest)
-    each(NC, gather.drain)
-
-    @pl.when(p.c != p.zl)
-    def _():
-        each(NC, lambda t: swap(t).wait_send())
-
-    for d in range(2):
-        weights.whole(d).wait_send()
 
 
 def lanes(rows):
@@ -390,15 +300,16 @@
     return jnp.where(lane < 64, outs[0], outs[1]).astype(BF)
 
 
-PROJECT, NEAR, FINISH = 2, 4, 6
-ENTER, RELAY, FAR, COMPUTE = 9, 11, 13, 15
-PROJECT2, NEAR2, FINISH2 = 17, 19, 21
-RELAY2, FAR2, COMPUTE2 = 23, 25, 27
-PROJECT3, NEAR3, FINISH3 = 29, 31, 33
-
-
-def tail(
-    qkv, own, mod, so, tw, to, hw, ow, out,
+PROJECT, NEAR, FINISH = 1, 3, 5
+ENTER, RELAY, FAR, COMPUTE = 8, 10, 12, 13
+PROJECT2, NEAR2, FINISH2 = 14, 16, 18
+RELAY2, FAR2, COMPUTE2 = 20, 22, 23
+PROJECT3, NEAR3, FINISH3 = 24, 26, 28
+
+
+def block(
+    latent, mod, sw, so, tw, to, hw, ow, out,
+    qkv, full0, nrm, mine0, theirs0, g0, h0, zs, zr, zl_, ls0, ss0, sr0,
     vx, ws, one, full1, mine, theirs, wt, full2, w1, w2, res, part,
     a1, fs1, fr1, ns1, nr1, a2, fs2, fr2, ns2, nr2, a3, fs3, fr3, ns3, nr3,
     s1, v1, s2, v2, s3, v3, g1, h1, g2, h2,
@@ -407,6 +318,8 @@
     p = Place()
     greet([p.L, p.R, p.D, p.S] + [p.row_dev(lax.rem(p.row + k, 16)) for k in range(1, 16)])
     here = blk(p.x, p.c)
+    wsq = QKV(p, sw, mine0, theirs0, zs, zr, zl_)
+    gat0 = Gather(p, full0, flat_rows, g0, h0)
     wso = Out(p, so, ws, 128, ps, pr, pl_)
     wtq = QKV(p, tw, mine, theirs, qs, qr, ql)
     wto = Out(p, to, wt, 128, us, ur, ul)
@@ -418,10 +331,95 @@
     gat1 = Gather(p, full1, flat_rows, g1, h1)
     gat2 = Gather(p, full2, flat_rows, g2, h2)
 
+    def eight(t, row):
+        return pl.ds(pl.multiple_of(t * CH + row * 8, 8), 8)
+
+    def strip(t, row):
+        return pl.ds(pl.multiple_of(row * 64 + t * 8, 8), 8)
+
+    def keep(t):
+        each(16, lambda k: pltpu.make_async_copy(latent.at[strip(t, k), :], full0.at[eight(t, k), here], ls0.at[t]).start())
+
+    def kept(t):
+        r = rows_of(t)
+        return pltpu.make_async_copy(latent.at[r, :], full0.at[r, here], ls0.at[t])
+
+    def swap(t):
+        there = blk(p.x, p.o)
+        each(
+            16,
+            lambda k: rc(
+                latent.at[strip(t, k), :], full0.at[eight(t, k), there], ss0.at[t], sr0.at[t], p.S
+            ).start(),
+        )
+
+    def swapped(t):
+        r = rows_of(t)
+        return rc(latent.at[r, :], full0.at[r, here], ss0.at[t], sr0.at[t], p.S)
+
+    @pl.when(p.c == p.zl)
+    def _():
+        each(NC, keep)
+
+    @pl.when(p.c != p.zl)
+    def _():
+        each(NC, swap)
+
+    for copy in wsq.locals():
+        copy.start()
+    each(NC, wsq.piece)
     each(4, wso.piece)
     for weights in (wso, wtq, wto, whi, wou):
         for copy in weights.locals():
             copy.start()
+
+    def first(t):
+        @pl.when(p.c == p.zl)
+        def _():
+            kept(t).wait()
+
+        @pl.when(p.c != p.zl)
+        def _():
+            swapped(t).wait_recv()
+
+        gat0.own(t)
+
+    def spatial(t):
+        @pl.when(t == 0)
+        def _():
+            for copy in wsq.locals():
+                copy.wait()
+
+        gat0.arrive(t)
+        r = rows_of(t)
+        nrm[r, :] = normed(full0[r, :], mod, 0)
+        qkv[r, 0:384] = jnp.dot(nrm[r, :], mine0[...], preferred_element_type=F32).astype(BF)
+
+    def spatial_rest(t):
+        @pl.when(t == 0)
+        def _():
+            for d in range(2):
+                wsq.whole(d).wait_recv()
+
+        r = rows_of(t)
+        qkv[r, 384:768] = jnp.dot(nrm[r, :], theirs0[...], preferred_element_type=F32).astype(BF)
+
+    def steps(total, *entries):
+        def body(i, carry):
+            for start, count, function in entries:
+
+                @pl.when((i >= start) & (i < start + count))
+                def _(t=i - start, function=function):
+                    function(t)
+
+            return carry
+
+        lax.fori_loop(0, total, body, 0)
+
+    steps(
+        NC + 10,
+        (0, NC, first), (2, NC, gat0.relay), (4, NC, gat0.far), (6, 8, wtq.piece), (6, NC, spatial), (10, NC, spatial_rest),
+    )
     for pair in range(2):
         vx[pair, :, 0:128] = qkv[:, pair * 384 + 256 : pair * 384 + 384]
         vx[pair, :, 128:256] = jnp.ones((T, 128), BF)
@@ -441,9 +439,6 @@
 
         r1.project(t)
 
-    def eight(t, row):
-        return pl.ds(pl.multiple_of(t * CH + row * 8, 8), 8)
-
     def cross(k, t):
         row = lax.rem(p.row + k, 16)
         return rc(one.at[eight(t, row), :], full1.at[eight(t, p.row), here], xs.at[k, t], xr.at[p.row, t], p.row_dev(row))
@@ -454,7 +449,7 @@
     def finish1(t):
         r = rows_of(t)
         gate = mod[2:3, here]
-        one[r, :] = (own[r, :].astype(F32) + gate * r1.total(t)).astype(BF)
+        one[r, :] = (full0[r, here].astype(F32) + gate * r1.total(t)).astype(BF)
         each(15, lambda k: cross(k + 1, t).start())
         stay(t).start()
 
@@ -522,10 +517,16 @@
         r3.project(t)
 
     def put(t):
+        each(16, lambda k: pltpu.make_async_copy(res.at[eight(t, k), :], out.at[strip(t, k), :], ls.at[t]).start())
+
+    def putted(t):
         r = rows_of(t)
         return pltpu.make_async_copy(res.at[r, :], out.at[r, :], ls.at[t])
 
     def back(t):
+        each(16, lambda k: rc(res.at[eight(t, k), :], out.at[strip(t, k), :], ss.at[t], sr.at[t], p.S).start())
+
+    def backed(t):
         r = rows_of(t)
         return rc(res.at[r, :], out.at[r, :], ss.at[t], sr.at[t], p.S)
 
@@ -536,23 +537,11 @@
 
         @pl.when(p.c == p.zl)
         def _():
-            put(t).start()
+            put(t)
 
         @pl.when(p.c != p.zl)
         def _():
-            back(t).start()
-
-    def steps(*entries):
-        def body(i, carry):
-            for first, count, function in entries:
-
-                @pl.when((i >= first) & (i < first + count))
-                def _(t=i - first, function=function):
-                    function(t)
-
-            return carry
-
-        lax.fori_loop(0, NC + FINISH3, body, 0)
+            back(t)
 
     def twice(piece):
         def run(i):
@@ -562,7 +551,8 @@
         return run
 
     steps(
-        (0, 8, wtq.piece), (8, 4, wto.piece), (12, 8, twice(whi.piece)), (20, 8, twice(wou.piece)),
+        NC + FINISH3,
+        (0, 4, wto.piece), (2, 3, twice(whi.piece)), (5, 10, lambda i: whi.piece(i + 6)), (15, 8, twice(wou.piece)),
         (FINISH, NC, finish1), (ENTER, NC, enter1), (RELAY, NC, gat1.relay), (FAR, NC, gat1.far),
         (NEAR, NC, r1.near), (NEAR2, NC, r2.near), (NEAR3, NC, r3.near),
         (FINISH2, NC, finish2), (RELAY2, NC, gat2.relay), (FAR2, NC, gat2.far), (FINISH3, NC, finish3),
@@ -571,22 +561,26 @@
     )
 
     def drain(t):
-        for stage in (r1, r2, r3, gat1, gat2):
+        for stage in (r1, r2, r3, gat0, gat1, gat2):
             stage.drain(t)
         each(15, lambda k: cross(k + 1, t).wait_send())
 
     each(NC, drain)
-    for weights in (wso, wtq, wto, whi, wou):
+    for weights in (wsq, wso, wtq, wto, whi, wou):
         for d in range(2):
             weights.whole(d).wait_send()
 
+    @pl.when(p.c != p.zl)
+    def _():
+        each(NC, lambda t: swapped(t).wait_send())
+
     @pl.when(p.c == p.zl)
     def _():
-        each(NC, lambda t: put(t).wait())
+        each(NC, lambda t: putted(t).wait())
 
     @pl.when(p.c != p.zl)
     def _():
-        each(NC, lambda t: back(t).wait())
+        each(NC, lambda t: backed(t).wait())
 
 
 def call(kernel, name, ident, ins, outs, scratch, limit, cost):
@@ -606,7 +600,7 @@
 
 def input_scratch():
     return [
-        VM((T, D), BF), VM((T, D), BF), VM((D, 384), BF), VM((D, 384), BF),
+        VM((T, 768), BF), VM((T, D), BF), VM((T, D), BF), VM((D, 384), BF), VM((D, 384), BF),
         DMA((9, NC)), DMA((9, NC)), DMA((2,)), DMA((2,)), DMA((3,)), DMA((NC,)), DMA((NC,)), DMA((NC,)),
     ]
 
@@ -626,15 +620,11 @@
     )
 
 
-def per_device(latent, mod, sqkv, so, tqkv, to, hw, ow):
-    tokens = latent.reshape(16, 8, 8, B).transpose(1, 0, 2, 3).reshape(T, B)
-    qkv, own = call(
-        spatial_in, "spatial_in", 0, [ANY, INV, ANY], [((T, 768), INV), ((T, B), INV)], input_scratch(), 60, 10**10
-    )(tokens, mod, sqkv)
+def per_device(latent, mod, *weights):
     (out,) = call(
-        tail, "tail", 1, [INV, INV, INV] + [ANY] * 5, [((T, B), ANY)], tail_scratch(), 60, 4 * 10**10
-    )(qkv, own, mod, so, tqkv, to, hw, ow)
-    return out.reshape(8, 16, 8, B).transpose(1, 0, 2, 3).reshape(16, 64, B)
+        block, "block", 0, [ANY, INV] + [ANY] * 6, [((T, B), ANY)], input_scratch() + tail_scratch(), 63, 4 * 10**10
+    )(latent.reshape(T, B), mod, *weights)
+    return out.reshape(16, 64, B)
 
 
 def solution(mesh):

time: 169 us -> 173 us (1.024)
  Pallas kernels: 165 us -> 171 us
  local copies, waits for them, and re-layouts: 3.76 us -> 1.88 us
    pallas_call x2 -> x1, Pallas kernels: 165 us -> 171 us  [per_device(): call(block, 'block', 0, [ANY, INV] + [ANY] * 6, [((T, B), ANY)], input_sc...]
    transpose x1 -> x0, local copies, waits for them, and re-layouts: 1.89 us -> none  [per_device(): return out.reshape(8, 16, 8, B).transpose(1, 0, 2, 3).reshape(16, 64, B)]
    unnamed x0 -> x1, local copies, waits for them, and re-layouts: none -> 1.88 us
    reshape x1 -> x0, local copies, waits for them, and re-layouts: 1.87 us -> none  [per_device(): tokens = latent.reshape(16, 8, 8, B).transpose(1, 0, 2, 3).reshape(T, B)]
where the time goes in v4:
time: 173 us; the launch traced here: 172 us
  Pallas kernels  171 us (99%)
  local copies, waits for them, and re-layouts  1.88 us (1%)
    pallas_call x1, Pallas kernels, per_device(): call(block, 'block', 0, [ANY, INV] + [ANY] * 6, [((T, B), ANY)], input_sc...  171 us

profile of v4, /device:TPU:1, one launch (start us, length us, event | category | flops | bytes accessed | tf_op | source)
XLA Modules:
  0.0 172.4 jit_solution(2212945602088509099)
XLA Ops:
  0.0 170.5 %block.1 = bf16[1024,256]{1,0:T(8,128)(2,1)} custom-call(bf16[1024,256]{1,0:T(8,128)(2,1)} %bitcast.3, f32[9,2048]{1,0:T(8,128)} %mod.1, bf16[3,2048,256]{2,1,0:T(8,128)(2,1)} %sw.1, bf16[256,2048]{1,0:T(8,128)(2,1)} %so.1, bf16[3,2048,256]{2,1,0:T(8,128)(2,1)} %tw.1, bf16[256,2048]{1,0:T(8,128)(2,1)} %to.1, bf16[2048,1024]{1,0:T(8,128)(2,1)} %hw.1, ...), custom_call_target="tpu_custom_call" | custom-call | flops 40000000000 | bytes 16777216 | tf_op jit(solution)/shard_map/block/pallas_call | solution.py:624
  170.6 1.9 %copy.10 = bf16[16,64,256]{2,1,0:T(8,128)(2,1)} copy(bf16[16,64,256]{2,1,0:T(8,128)(2,1)} %bitcast.2) | data formatting | bytes 1048576

commit v5 on v4

--- a/solution.py
+++ b/solution.py
@@ -305,6 +305,7 @@
 PROJECT2, NEAR2, FINISH2 = 14, 16, 18
 RELAY2, FAR2, COMPUTE2 = 20, 22, 23
 PROJECT3, NEAR3, FINISH3 = 24, 26, 28
+PLAN = ((1, 4, 1), (5, 4, 1), (9, 4, 2), (13, 10, 2))
 
 
 def block(
@@ -543,16 +544,39 @@
         def _():
             back(t)
 
-    def twice(piece):
-        def run(i):
-            piece(2 * i)
-            piece(2 * i + 1)
-
-        return run
+    def pace(plan):
+        order = [(wto, n) for n in range(4)] + [(whi, n) for n in range(16)] + [(wou, n) for n in range(16)]
+        runs = []
+        for start, count, rate in plan:
+            for step in range(start, start + count):
+                for weights, n in order[:rate]:
+                    last = runs[-1] if runs else None
+                    if last and last[0] is weights and last[2] == rate and (n - last[3]) // rate == step - last[1]:
+                        last[4] = n + 1
+                    else:
+                        runs.append([weights, step, rate, n, n + 1])
+                order = order[rate:]
+        assert not order
+
+        def entry(weights, step, rate, low, high):
+            def run(i):
+                for k in range(rate):
+                    n = low + rate * i + k
+                    if (high - low) % rate == 0:
+                        weights.piece(n)
+                    else:
+
+                        @pl.when(n < high)
+                        def _(n=n):
+                            weights.piece(n)
+
+            return step, -(-(high - low) // rate), run
+
+        return [entry(*run) for run in runs]
 
     steps(
         NC + FINISH3,
-        (0, 4, wto.piece), (2, 3, twice(whi.piece)), (5, 10, lambda i: whi.piece(i + 6)), (15, 8, twice(wou.piece)),
+        *pace(PLAN),
         (FINISH, NC, finish1), (ENTER, NC, enter1), (RELAY, NC, gat1.relay), (FAR, NC, gat1.far),
         (NEAR, NC, r1.near), (NEAR2, NC, r2.near), (NEAR3, NC, r3.near),
         (FINISH2, NC, finish2), (RELAY2, NC, gat2.relay), (FAR2, NC, gat2.far), (FINISH3, NC, finish3),

time: 173 us -> 164 us (0.948)
  Pallas kernels: 171 us -> 162 us
    pallas_call x1, Pallas kernels: 171 us -> 162 us  [per_device(): call(block, 'block', 0, [ANY, INV] + [ANY] * 6, [((T, B), ANY)], input_sc...]
where the time goes in v5:
time: 164 us
  Pallas kernels  162 us (99%)
  local copies, waits for them, and re-layouts  1.88 us (1%)
    pallas_call x1, Pallas kernels, per_device(): call(block, 'block', 0, [ANY, INV] + [ANY] * 6, [((T, B), ANY)], input_sc...  162 us

profile of v5, /device:TPU:1, one launch (start us, length us, event | category | flops | bytes accessed | tf_op | source)
XLA Modules:
  0.0 163.8 jit_solution(11716659386526727587)
XLA Ops:
  0.0 161.9 %block.1 = bf16[1024,256]{1,0:T(8,128)(2,1)} custom-call(bf16[1024,256]{1,0:T(8,128)(2,1)} %bitcast.3, f32[9,2048]{1,0:T(8,128)} %mod.1, bf16[3,2048,256]{2,1,0:T(8,128)(2,1)} %sw.1, bf16[256,2048]{1,0:T(8,128)(2,1)} %so.1, bf16[3,2048,256]{2,1,0:T(8,128)(2,1)} %tw.1, bf16[256,2048]{1,0:T(8,128)(2,1)} %to.1, bf16[2048,1024]{1,0:T(8,128)(2,1)} %hw.1, ...), custom_call_target="tpu_custom_call" | custom-call | flops 40000000000 | bytes 16777216 | tf_op jit(solution)/shard_map/block/pallas_call | solution.py:648
  161.9 1.9 %copy.10 = bf16[16,64,256]{2,1,0:T(8,128)(2,1)} copy(bf16[16,64,256]{2,1,0:T(8,128)(2,1)} %bitcast.2) | data formatting | bytes 1048576

commit v6 on v5

--- a/solution.py
+++ b/solution.py
@@ -576,12 +576,11 @@
 
     steps(
         NC + FINISH3,
-        *pace(PLAN),
-        (FINISH, NC, finish1), (ENTER, NC, enter1), (RELAY, NC, gat1.relay), (FAR, NC, gat1.far),
         (NEAR, NC, r1.near), (NEAR2, NC, r2.near), (NEAR3, NC, r3.near),
+        (FINISH, NC, finish1), (RELAY, NC, gat1.relay), (FAR, NC, gat1.far),
         (FINISH2, NC, finish2), (RELAY2, NC, gat2.relay), (FAR2, NC, gat2.far), (FINISH3, NC, finish3),
-        (PROJECT, NC, project1), (PROJECT2, NC, project2), (PROJECT3, NC, project3),
-        (0, NC, heads), (COMPUTE, NC, temporal), (COMPUTE2, NC, hidden),
+        (PROJECT, NC, project1), (PROJECT2, NC, project2), (PROJECT3, NC, project3), (ENTER, NC, enter1),
+        *pace(PLAN), (0, NC, heads), (COMPUTE, NC, temporal), (COMPUTE2, NC, hidden),
     )
 
     def drain(t):

time: 164 us -> 162 us (0.988)
  Pallas kernels: 162 us -> 160 us
    pallas_call x1, Pallas kernels: 162 us -> 160 us  [per_device(): call(block, 'block', 0, [ANY, INV] + [ANY] * 6, [((T, B), ANY)], input_sc...]
where the time goes in v6:
time: 162 us; the launch traced here: 161 us
  Pallas kernels  160 us (99%)
  local copies, waits for them, and re-layouts  1.88 us (1%)
    pallas_call x1, Pallas kernels, per_device(): call(block, 'block', 0, [ANY, INV] + [ANY] * 6, [((T, B), ANY)], input_sc...  160 us

profile of v6, /device:TPU:1, one launch (start us, length us, event | category | flops | bytes accessed | tf_op | source)
XLA Modules:
  0.0 161.4 jit_solution(13980045119684665020)
XLA Ops:
  0.0 159.6 %block.1 = bf16[1024,256]{1,0:T(8,128)(2,1)} custom-call(bf16[1024,256]{1,0:T(8,128)(2,1)} %bitcast.3, f32[9,2048]{1,0:T(8,128)} %mod.1, bf16[3,2048,256]{2,1,0:T(8,128)(2,1)} %sw.1, bf16[256,2048]{1,0:T(8,128)(2,1)} %so.1, bf16[3,2048,256]{2,1,0:T(8,128)(2,1)} %tw.1, bf16[256,2048]{1,0:T(8,128)(2,1)} %to.1, bf16[2048,1024]{1,0:T(8,128)(2,1)} %hw.1, ...), custom_call_target="tpu_custom_call" | custom-call | flops 40000000000 | bytes 16777216 | tf_op jit(solution)/shard_map/block/pallas_call | solution.py:647
  159.6 1.9 %copy.10 = bf16[16,64,256]{2,1,0:T(8,128)(2,1)} copy(bf16[16,64,256]{2,1,0:T(8,128)(2,1)} %bitcast.2) | data formatting | bytes 1048576

commit v7 on v6

--- a/solution.py
+++ b/solution.py
@@ -305,7 +305,7 @@
 PROJECT2, NEAR2, FINISH2 = 14, 16, 18
 RELAY2, FAR2, COMPUTE2 = 20, 22, 23
 PROJECT3, NEAR3, FINISH3 = 24, 26, 28
-PLAN = ((1, 4, 1), (5, 4, 1), (9, 4, 2), (13, 10, 2))
+PLAN = ((0, 10, 1), (10, 13, 2))
 
 
 def block(
@@ -418,8 +418,8 @@
         lax.fori_loop(0, total, body, 0)
 
     steps(
-        NC + 10,
-        (0, NC, first), (2, NC, gat0.relay), (4, NC, gat0.far), (6, 8, wtq.piece), (6, NC, spatial), (10, NC, spatial_rest),
+        NC + 9,
+        (0, NC, first), (2, NC, gat0.relay), (4, NC, gat0.far), (6, 8, wtq.piece), (5, NC, spatial), (9, NC, spatial_rest),
     )
     for pair in range(2):
         vx[pair, :, 0:128] = qkv[:, pair * 384 + 256 : pair * 384 + 384]

time: 162 us -> 164 us (1.012)
    pallas_call x1, Pallas kernels: 160 us -> 161 us  [per_device(): call(block, 'block', 0, [ANY, INV] + [ANY] * 6, [((T, B), ANY)], input_sc...]
where the time goes in v7:
time: 164 us; the launch traced here: 163 us
  Pallas kernels  161 us (98%)
  local copies, waits for them, and re-layouts  1.88 us (1%)
    pallas_call x1, Pallas kernels, per_device(): call(block, 'block', 0, [ANY, INV] + [ANY] * 6, [((T, B), ANY)], input_sc...  161 us

profile of v7, /device:TPU:1, one launch (start us, length us, event | category | flops | bytes accessed | tf_op | source)
XLA Modules:
  0.0 163.4 jit_solution(10597968156184217680)
XLA Ops:
  0.0 161.5 %block.1 = bf16[1024,256]{1,0:T(8,128)(2,1)} custom-call(bf16[1024,256]{1,0:T(8,128)(2,1)} %bitcast.3, f32[9,2048]{1,0:T(8,128)} %mod.1, bf16[3,2048,256]{2,1,0:T(8,128)(2,1)} %sw.1, bf16[256,2048]{1,0:T(8,128)(2,1)} %so.1, bf16[3,2048,256]{2,1,0:T(8,128)(2,1)} %tw.1, bf16[256,2048]{1,0:T(8,128)(2,1)} %to.1, bf16[2048,1024]{1,0:T(8,128)(2,1)} %hw.1, ...), custom_call_target="tpu_custom_call" | custom-call | flops 40000000000 | bytes 16777216 | tf_op jit(solution)/shard_map/block/pallas_call | solution.py:647
  161.5 1.9 %copy.10 = bf16[16,64,256]{2,1,0:T(8,128)(2,1)} copy(bf16[16,64,256]{2,1,0:T(8,128)(2,1)} %bitcast.2) | data formatting | bytes 1048576
